TPU v7x, 32 devices: a whole 2x2x4 slice. The times are simulated.
32 devices in a mesh: cp: 8 (over y, x, core), grp: 4 (over z).
Axes of the slice: x: 2, y: 2, z: 4, core: 2. Of those that a mesh axis runs over, the one named last changes fastest.
Arguments:
- queries: bfloat16 [4096, 2048], P(('cp', 'grp')), may hold values from -6 to 6
- keys: bfloat16 [4096, 512], P(('cp', 'grp')), may hold values from -6 to 6
- values: bfloat16 [4096, 512], P(('cp', 'grp')), may hold values from -6 to 6
- grad_out: bfloat16 [4096, 2048], P(('cp', 'grp')), may hold values from -6 to 6
- segments: int32 [4096], P(('cp', 'grp')), may hold values from 0 to 3, never falling along the last dimension, each value on 1 to 2048 neighbouring positions
- block_ids: int32 [32, 4], P(('cp', 'grp')), may hold values from 0 to 31, as said below
- block_count: int32 [32], P(('cp', 'grp')), may hold values from 1 to 4, as said below
Outputs:
- attended: bfloat16 [4096, 2048], P(('cp', 'grp'))
- grad_queries: bfloat16 [4096, 2048], P(('cp', 'grp'))
- grad_keys: bfloat16 [4096, 512], P(('cp', 'grp'))
- grad_values: bfloat16 [4096, 512], P(('cp', 'grp'))
Inputs may be any that keep to these rules, and one draw needn't show every extreme that they name: `block_ids`: row t names tiles of its own neighbourhood (tiles 4 * (t // 4) onward, 4 of them) or of the neighbourhood before it; entry 0 is t itself; the first block_count[t] entries are distinct; later entries are ignored. `block_count`: reaches 4 in every draw.
All inputs are finite; a program needn't handle non-finite values.
Results may differ from a plain program's by a relative error of at most 0.012.
The roundings to bfloat16 on the way count: a program that leaves them out, or rounds other values in their place, can miss the bound.
Values may be sent and summed in bfloat16 or wider, within the bound.
No kernel may reach another device: no remote copies, remote signals or barrier semaphores. Data moves between devices by JAX's collectives and lax.ppermute only.
A program may use at most 64 MiB of HBM per device.

v0:
```python
import jax
import jax.numpy as jnp
from jax import lax
from jax.sharding import PartitionSpec as P

KV_HEADS = 4


NEG = -1e30


def from_behind(value, axis, steps):
    count = lax.axis_size(axis)
    initial, last = (max(0, -steps), min(count, count - steps))
    return lax.ppermute(value, axis, [(source, source + steps) for source in range(initial, last)])


def attend_tile(query, grad_out, tile_keys, tile_values, query_seg, key_seg, is_live, kv_heads):
    tile_rows, full_width = query.shape
    slot_count, tile_size, kv_width = tile_keys.shape
    head_size = kv_width // kv_heads
    group_size = full_width // kv_width
    scaling = head_size ** (-0.5)
    key_slots = slot_count * tile_size
    allowed = (query_seg[:, None] == key_seg.reshape(key_slots)[None, :]) & jnp.repeat(
        is_live, tile_size
    )[None, :]
    query_heads = query.reshape(tile_rows, kv_heads, group_size, head_size).transpose(1, 0, 2, 3)
    grad_heads = grad_out.reshape(tile_rows, kv_heads, group_size, head_size).transpose(1, 0, 2, 3)
    key_heads = tile_keys.reshape(key_slots, kv_heads, head_size).transpose(1, 0, 2)
    value_heads = tile_values.reshape(key_slots, kv_heads, head_size).transpose(1, 0, 2)

    def per_head(pieces):
        query_one, grad_one, key_one, value_one = pieces
        scores = (
            jnp.einsum("bge,ne->gbn", query_one, key_one, preferred_element_type=jnp.float32)
            * scaling
        )
        scores = jnp.where(allowed[None], scores, NEG)
        probability = jnp.exp(scores - jnp.max(scores, axis=-1, keepdims=True))
        probability = probability / jnp.sum(probability, axis=-1, keepdims=True)
        weights = probability.astype(jnp.bfloat16)
        attended = jnp.einsum(
            "gbn,ne->bge", weights, value_one, preferred_element_type=jnp.float32
        ).astype(jnp.bfloat16)
        row_delta = jnp.sum(
            lax.optimization_barrier(attended).astype(jnp.float32) * grad_one.astype(jnp.float32),
            axis=-1,
        )
        dprobs = jnp.einsum("bge,ne->gbn", grad_one, value_one, preferred_element_type=jnp.float32)
        dscores = (probability * (dprobs - row_delta.T[:, :, None])).astype(jnp.bfloat16)
        grad_query = (
            jnp.einsum("gbn,ne->bge", dscores, key_one, preferred_element_type=jnp.float32)
            * scaling
        ).astype(jnp.bfloat16)
        key_term = (
            jnp.einsum("gbn,bge->ne", dscores, query_one, preferred_element_type=jnp.float32)
            * scaling
        )
        value_term = jnp.einsum(
            "gbn,bge->ne", weights, grad_one, preferred_element_type=jnp.float32
        )
        return (attended, grad_query, key_term, value_term)

    attended, grad_query, key_term, value_term = lax.map(
        per_head, (query_heads, grad_heads, key_heads, value_heads)
    )
    attended = attended.transpose(1, 0, 2, 3).reshape(tile_rows, full_width)
    grad_query = grad_query.transpose(1, 0, 2, 3).reshape(tile_rows, full_width)
    key_term = key_term.transpose(1, 0, 2).reshape(slot_count, tile_size, kv_width)
    value_term = value_term.transpose(1, 0, 2).reshape(slot_count, tile_size, kv_width)
    return (attended, grad_query, key_term, value_term)


def add_sources(received, group_size, tile_size, kv_width):
    return jnp.sum(received.astype(jnp.float32).reshape(group_size, tile_size, kv_width), axis=0)


def pick_slots(far_part, near_part, is_far, far_index, near_index):
    chosen_far = far_part[far_index]
    chosen_near = near_part[near_index]
    shape_tail = (1,) * (chosen_far.ndim - 1)
    return jnp.where(is_far.reshape((-1,) + shape_tail), chosen_far, chosen_near)


def place_terms(terms, mask, index, group_size):
    kept = jnp.where(mask[:, None, None], terms, jnp.zeros_like(terms))
    empty = jnp.zeros((group_size,) + terms.shape[1:], jnp.float32)
    return empty.at[index].add(kept).reshape(group_size * terms.shape[1], terms.shape[2])


def body(queries, keys, values, grad_out, segments, block_ids, block_count):
    tile_size = queries.shape[0]
    kv_width = keys.shape[1]
    group_size = lax.axis_size("grp")
    near_keys, near_values, near_segs = (
        lax.all_gather(keys, "grp", axis=0, tiled=True),
        lax.all_gather(values, "grp", axis=0, tiled=True),
        lax.all_gather(segments, "grp", axis=0, tiled=True),
    )
    far_keys, far_values, far_segs = from_behind((near_keys, near_values, near_segs), "cp", 1)
    first_id = (lax.axis_index("cp") - 1) * group_size
    pool_slot = jnp.clip(block_ids[0] - first_id, 0, 2 * group_size - 1)
    is_far = pool_slot < group_size
    far_index = jnp.clip(pool_slot, 0, group_size - 1)
    near_index = jnp.clip(pool_slot - group_size, 0, group_size - 1)
    tile_keys = pick_slots(
        far_keys.reshape(group_size, tile_size, kv_width),
        near_keys.reshape(group_size, tile_size, kv_width),
        is_far,
        far_index,
        near_index,
    )
    tile_values = pick_slots(
        far_values.reshape(group_size, tile_size, kv_width),
        near_values.reshape(group_size, tile_size, kv_width),
        is_far,
        far_index,
        near_index,
    )
    tile_segs = pick_slots(
        far_segs.reshape(group_size, tile_size),
        near_segs.reshape(group_size, tile_size),
        is_far,
        far_index,
        near_index,
    )
    is_live = jnp.arange(block_ids.shape[1], dtype=jnp.int32) < block_count[0]
    attended, grad_query, key_term, value_term = attend_tile(
        queries, grad_out, tile_keys, tile_values, segments, tile_segs, is_live, KV_HEADS
    )
    key_low = key_term.astype(jnp.bfloat16).astype(jnp.float32)
    value_low = value_term.astype(jnp.bfloat16).astype(jnp.float32)
    is_near = jnp.logical_not(is_far)
    far_dkeys = place_terms(key_low, is_far, far_index, group_size)
    far_dvalues = place_terms(value_low, is_far, far_index, group_size)
    near_dkeys = place_terms(key_low, is_near, near_index, group_size)
    near_dvalues = place_terms(value_low, is_near, near_index, group_size)
    got_far_keys, got_far_values, got_near_keys, got_near_values = (
        lax.all_to_all(
            far_dkeys.astype(jnp.bfloat16), "grp", split_axis=0, concat_axis=0, tiled=True
        ),
        lax.all_to_all(
            far_dvalues.astype(jnp.bfloat16), "grp", split_axis=0, concat_axis=0, tiled=True
        ),
        lax.all_to_all(
            near_dkeys.astype(jnp.bfloat16), "grp", split_axis=0, concat_axis=0, tiled=True
        ),
        lax.all_to_all(
            near_dvalues.astype(jnp.bfloat16), "grp", split_axis=0, concat_axis=0, tiled=True
        ),
    )
    far_sum_keys = add_sources(got_far_keys, group_size, tile_size, kv_width)
    far_sum_values = add_sources(got_far_values, group_size, tile_size, kv_width)
    near_sum_keys = add_sources(got_near_keys, group_size, tile_size, kv_width)
    near_sum_values = add_sources(got_near_values, group_size, tile_size, kv_width)
    later_keys, later_values = (
        from_behind(far_sum_keys.astype(jnp.bfloat16), "cp", -1).astype(far_sum_keys.dtype),
        from_behind(far_sum_values.astype(jnp.bfloat16), "cp", -1).astype(far_sum_values.dtype),
    )
    grad_keys = (near_sum_keys + later_keys).astype(jnp.bfloat16)
    grad_values = (near_sum_values + later_values).astype(jnp.bfloat16)
    return (attended, grad_query, grad_keys, grad_values)


def solution(mesh):
    placed = (
        P(("cp", "grp"), None),
        P(("cp", "grp"), None),
        P(("cp", "grp"), None),
        P(("cp", "grp"), None),
        P(("cp", "grp")),
        P(("cp", "grp"), None),
        P(("cp", "grp")),
    )
    return jax.shard_map(
        body,
        mesh=mesh,
        in_specs=placed,
        out_specs=(
            P(("cp", "grp"), None),
            P(("cp", "grp"), None),
            P(("cp", "grp"), None),
            P(("cp", "grp"), None),
        ),
        check_vma=False,
    )
```

profile of v0, /device:TPU:0, one launch (start us, length us, event | category | flops | bytes accessed | tf_op | source)
XLA Modules:
  0.0 187.7 jit_solution(12074125178734897156)
XLA Ops:
  0.6 17.7 %all_gather.11 = bf16[512,512]{1,0:T(8,128)(2,1)S(1)} all-gather(bf16[128,512]{1,0:T(8,128)(2,1)} %param.10), channel_id=1, replica_groups=mesh['cp'=8,'grp'=4] {'grp'}, dimensions={0}, use_global_device_ids=true | all-gather | bytes 655360 | tf_op jit(solution)/shard_map/all_gather | solution.py:97
  18.4 2.1 %collective-permute-start.2 = (bf16[512,512]{1,0:T(8,128)(2,1)S(1)}, bf16[512,512]{1,0:T(8,128)(2,1)}, u32[]{:S(2)}, u32[]{:S(2)}) collective-permute-start(bf16[512,512]{1,0:T(8,128)(2,1)S(1)} %all_gather.11), channel_id=1, source_target_pairs={{0,4},{4,8},{8,12},{12,16},{16,20},{20,24},{24,28},{1,5},{5,9},{9,... | collective-permute-start | bytes 1572872 | tf_op jit(solution)/shard_map/ppermute | solution.py:15
  20.4 17.2 %all_gather.9 = bf16[512,512]{1,0:T(8,128)(2,1)S(1)} all-gather(bf16[128,512]{1,0:T(8,128)(2,1)S(1)} %copy-done.9), channel_id=1, replica_groups=mesh['cp'=8,'grp'=4] {'grp'}, dimensions={0}, use_global_device_ids=true | all-gather | bytes 655360 | tf_op jit(solution)/shard_map/all_gather | solution.py:98
  37.7 3.0 %collective-permute-start = (bf16[512,512]{1,0:T(8,128)(2,1)S(1)}, bf16[512,512]{1,0:T(8,128)(2,1)}, u32[]{:S(2)}, u32[]{:S(2)}) collective-permute-start(bf16[512,512]{1,0:T(8,128)(2,1)S(1)} %all_gather.9), channel_id=1, source_target_pairs={{0,4},{4,8},{8,12},{12,16},{16,20},{20,24},{24,28},{1,5},{5,9},{9,... | collective-permute-start | bytes 1572872 | tf_op jit(solution)/shard_map/ppermute | solution.py:15
  40.7 10.2 %all-gather = s32[4,1,128]{2,1,0:T(1,128)S(1)} all-gather(s32[1,1,128]{2,1,0:T(1,128)S(1)} %bitcast.234), channel_id=1, replica_groups=mesh['cp'=8,'grp'=4] {'grp'}, dimensions={0}, use_global_device_ids=true | all-gather | bytes 2560 | tf_op jit(solution)/shard_map/all_gather | solution.py:99
  58.8 1.6 gather_fusion.4
  61.4 1.6 gather_fusion
  64.1 3.8 %select_bitcast_fusion = (bf16[4,512,128]{2,0,1:T(4,128)(2,1)}, bf16[4,512,128]{2,0,1:T(4,128)(2,1)S(1)}) fusion(bf16[512,4,128]{2,1,0:T(4,128)(2,1)S(1)} %copy-done, bf16[512,4,128]{2,1,0:T(4,128)(2,1)S(1)} %gather.41, pred[512]{0:T(512)(128)(4,1)S(1)} %broadcast_bitcast_fusion.1, bf16[512,4,128]{2,1,0:T(4,128)(2,1)} %gather.31, ...), kind=kLoop, calls=%fused_computation.71 | loop fusion | flops 524288 | bytes 3146240 | tf_op jit(solution)/shard_map/transpose | solution.py:30
  69.9 30.3 %while.17 = (s32[]{:T(128)}, bf16[4,128,4,128]{1,3,2,0:T(8,128)(2,1)S(1)}, bf16[4,128,4,128]{1,3,2,0:T(8,128)(2,1)}, bf16[4,512,128]{2,1,0:T(8,128)(2,1)}, bf16[...) while((s32[]{:T(128)}, ...), condition=%wide.region_4.5_spmd.clone, body=%wide.region_0.4_spmd.clone.sunk | while | flops 542246912 | bytes 10902721 | solution.py:65
  70.1 1.4 fusion.118
  72.4 1.6 fusion.119
  77.7 1.4 fusion.118
  79.9 1.6 fusion.119
  83.7 1.3 fusion.122
  85.3 1.4 fusion.118
  87.5 1.6 fusion.119
  92.8 1.4 fusion.118
  95.1 1.6 fusion.119
  98.9 1.3 fusion.122
  100.2 1.5 convert_bitcast_fusion
  103.5 1.5 reshape.183
  105.0 3.3 %broadcast_select_fusion.2 = (f32[4,128,512]{2,1,0:T(8,128)}, f32[4,128,512]{2,1,0:T(8,128)}, f32[4,128,512]{2,1,0:T(8,128)S(1)}, f32[4,128,512]{2,1,0:T(8,128)S(1)}) fusion(f32[4,128,512]{2,1,0:T(8,128)S(1)} %reshape.182, pred[4]{0:T(512)(128)(4,1)S(1)} %get-tuple-element.153, pred[4]{0:T(512)(128)(4,1)S(1)} %get-tuple-element.152, f32[4,128,512]{2,1,0:T(8,128)} %reshape.183), kind=kLoop, calls=%fused_computation.69 | loop fusion | flops 1048576 | bytes 6291464 | tf_op jit(solution)/shard_map/jit(_where)/select_n | solution.py:87
  108.4 2.3 %scatter_fusion = f32[4,128,512]{2,1,0:T(8,128)S(1)} fusion(f32[4,128,512]{2,1,0:T(8,128)S(1)} %broadcast.199.clone, s32[4]{0:T(128)S(1)} %get-tuple-element.166, f32[4,128,512]{2,1,0:T(8,128)} %get-tuple-element.161), kind=kCustom, calls=%fused_computation.6 | custom fusion | flops 262144 | bytes 3145744 | tf_op jit(solution)/shard_map/scatter-add | solution.py:89
  111.6 4.1 %all-to-all-start = ((bf16[4,128,512]{2,1,0:T(8,128)(2,1)}), bf16[4,128,512]{2,1,0:T(8,128)(2,1)}, u32[]{:S(2)}, u32[]{:S(2)}) async-start(bf16[4,128,512]{2,1,0:T(8,128)(2,1)} %convert_element_type.98), calls=%async_computation | async-start | bytes 1048576 | tf_op jit(solution)/shard_map/all_to_all | solution.py:146
  115.9 2.3 %scatter_fusion.1 = f32[4,128,512]{2,1,0:T(8,128)S(1)} fusion(f32[4,128,512]{2,1,0:T(8,128)S(1)} %broadcast.199.clone.1, s32[4]{0:T(128)S(1)} %get-tuple-element.167, f32[4,128,512]{2,1,0:T(8,128)} %get-tuple-element.160), kind=kCustom, calls=%fused_computation.7 | custom fusion | flops 262144 | bytes 3145744 | tf_op jit(solution)/shard_map/scatter-add | solution.py:89
  119.0 12.0 %all-to-all-done = bf16[4,128,512]{2,1,0:T(8,128)(2,1)} async-done(((bf16[4,128,512]{2,1,0:T(8,128)(2,1)}), bf16[4,128,512]{2,1,0:T(8,128)(2,1)}, u32[]{:S(2)}, u32[]{:S(2)}) %all-to-all-start) | async-done | bytes 524320 | tf_op jit(solution)/shard_map/all_to_all | solution.py:146
  131.0 4.1 %all-to-all-start.1 = ((bf16[4,128,512]{2,1,0:T(8,128)(2,1)}), bf16[4,128,512]{2,1,0:T(8,128)(2,1)}, u32[]{:S(2)}, u32[]{:S(2)}) async-start(bf16[4,128,512]{2,1,0:T(8,128)(2,1)} %convert_element_type.100), calls=%async_computation.1 | async-start | bytes 1048576 | tf_op jit(solution)/shard_map/all_to_all | solution.py:140
  137.3 13.4 %all-to-all-done.1 = bf16[4,128,512]{2,1,0:T(8,128)(2,1)} async-done(((bf16[4,128,512]{2,1,0:T(8,128)(2,1)}), bf16[4,128,512]{2,1,0:T(8,128)(2,1)}, u32[]{:S(2)}, u32[]{:S(2)}) %all-to-all-start.1) | async-done | bytes 524320 | tf_op jit(solution)/shard_map/all_to_all | solution.py:140
  150.7 3.5 %all-to-all-start.3 = ((bf16[4,128,512]{2,1,0:T(8,128)(2,1)}), bf16[4,128,512]{2,1,0:T(8,128)(2,1)S(1)}, u32[]{:S(2)}, u32[]{:S(2)}) async-start(bf16[4,128,512]{2,1,0:T(8,128)(2,1)} %convert_element_type.109), calls=%async_computation.3 | async-start | bytes 1048576 | tf_op jit(solution)/shard_map/all_to_all | solution.py:143
  156.3 12.4 %all-to-all-done.3 = bf16[4,128,512]{2,1,0:T(8,128)(2,1)S(1)} async-done(((bf16[4,128,512]{2,1,0:T(8,128)(2,1)}), bf16[4,128,512]{2,1,0:T(8,128)(2,1)S(1)}, u32[]{:S(2)}, u32[]{:S(2)}) %all-to-all-start.3) | async-done | bytes 524320 | tf_op jit(solution)/shard_map/all_to_all | solution.py:143
  168.8 3.5 %all-to-all-start.2 = ((bf16[4,128,512]{2,1,0:T(8,128)(2,1)}), bf16[4,128,512]{2,1,0:T(8,128)(2,1)S(1)}, u32[]{:S(2)}, u32[]{:S(2)}) async-start(bf16[4,128,512]{2,1,0:T(8,128)(2,1)} %convert_element_type.107), calls=%async_computation.2 | async-start | bytes 1048576 | tf_op jit(solution)/shard_map/all_to_all | solution.py:149
  179.3 7.0 %all-to-all-done.2 = bf16[4,128,512]{2,1,0:T(8,128)(2,1)S(1)} async-done(((bf16[4,128,512]{2,1,0:T(8,128)(2,1)}), bf16[4,128,512]{2,1,0:T(8,128)(2,1)S(1)}, u32[]{:S(2)}, u32[]{:S(2)}) %all-to-all-start.2) | async-done | bytes 524320 | tf_op jit(solution)/shard_map/all_to_all | solution.py:149
  (111 shorter events, 43.0 us)
Async XLA Ops:
  0.6 19.8 %copy-start.9 = (bf16[128,512]{1,0:T(8,128)(2,1)S(1)}, bf16[128,512]{1,0:T(8,128)(2,1)}, u32[]{:S(2)}) copy-start(bf16[128,512]{1,0:T(8,128)(2,1)} %param.11) | copy-start | bytes 393220
  18.4 40.5 %collective-permute-start.2 = (bf16[512,512]{1,0:T(8,128)(2,1)S(1)}, bf16[512,512]{1,0:T(8,128)(2,1)}, u32[]{:S(2)}, u32[]{:S(2)}) collective-permute-start(bf16[512,512]{1,0:T(8,128)(2,1)S(1)} %all_gather.11), channel_id=1, source_target_pairs={{0,4},{4,8},{8,12},{12,16},{16,20},{20,24},{24,28},{1,5},{5,9},{9,... | collective-permute-start | bytes 1572872 | tf_op jit(solution)/shard_map/ppermute | solution.py:15
  37.7 3.0 %copy-start.10 = (s32[128]{0:T(128)S(1)}, s32[128]{0:T(128)}, u32[]{:S(2)}) copy-start(s32[128]{0:T(128)} %param.13) | copy-start | bytes 1540
  37.7 23.7 %collective-permute-start = (bf16[512,512]{1,0:T(8,128)(2,1)S(1)}, bf16[512,512]{1,0:T(8,128)(2,1)}, u32[]{:S(2)}, u32[]{:S(2)}) collective-permute-start(bf16[512,512]{1,0:T(8,128)(2,1)S(1)} %all_gather.9), channel_id=1, source_target_pairs={{0,4},{4,8},{8,12},{12,16},{16,20},{20,24},{24,28},{1,5},{5,9},{9,... | collective-permute-start | bytes 1572872 | tf_op jit(solution)/shard_map/ppermute | solution.py:15
  50.9 7.4 %collective-permute-start.1 = (s32[512]{0:T(512)S(1)}, s32[512]{0:T(512)S(1)}, u32[]{:S(2)}, u32[]{:S(2)}) collective-permute-start(s32[512]{0:T(512)S(1)} %bitcast.230), channel_id=1, source_target_pairs={{0,4},{4,8},{8,12},{12,16},{16,20},{20,24},{24,28},{1,5},{5,9},{9,... | collective-permute-start | bytes 6152 | tf_op jit(solution)/shard_map/ppermute | solution.py:15
  52.1 0.7 copy-start.11
  55.0 1.0 copy-start.2
  63.0 1.1 copy-start
  67.9 1.0 copy-start.1
  68.9 1.0 copy-start.3
  74.0 1.0 copy-start.7
  75.4 0.8 copy-start.8
  81.5 1.0 copy-start.7
  82.9 0.8 copy-start.8
  89.1 1.0 copy-start.7
  90.5 0.8 copy-start.8
  96.6 1.0 copy-start.7
  98.1 0.8 copy-start.8
  100.2 1.5 copy-start.4
  111.6 19.4 %all-to-all-start = ((bf16[4,128,512]{2,1,0:T(8,128)(2,1)}), bf16[4,128,512]{2,1,0:T(8,128)(2,1)}, u32[]{:S(2)}, u32[]{:S(2)}) async-start(bf16[4,128,512]{2,1,0:T(8,128)(2,1)} %convert_element_type.98), calls=%async_computation | async-start | bytes 1048576 | tf_op jit(solution)/shard_map/all_to_all | solution.py:146
  131.0 19.7 %all-to-all-start.1 = ((bf16[4,128,512]{2,1,0:T(8,128)(2,1)}), bf16[4,128,512]{2,1,0:T(8,128)(2,1)}, u32[]{:S(2)}, u32[]{:S(2)}) async-start(bf16[4,128,512]{2,1,0:T(8,128)(2,1)} %convert_element_type.100), calls=%async_computation.1 | async-start | bytes 1048576 | tf_op jit(solution)/shard_map/all_to_all | solution.py:140
  150.7 18.1 %all-to-all-start.3 = ((bf16[4,128,512]{2,1,0:T(8,128)(2,1)}), bf16[4,128,512]{2,1,0:T(8,128)(2,1)S(1)}, u32[]{:S(2)}, u32[]{:S(2)}) async-start(bf16[4,128,512]{2,1,0:T(8,128)(2,1)} %convert_element_type.109), calls=%async_computation.3 | async-start | bytes 1048576 | tf_op jit(solution)/shard_map/all_to_all | solution.py:143
  156.3 15.9 %copy-start.5 = (bf16[4,128,4,128]{1,3,2,0:T(8,128)(2,1)S(1)}, bf16[4,128,4,128]{1,3,2,0:T(8,128)(2,1)}, u32[]{:S(2)}) copy-start(bf16[4,128,4,128]{1,3,2,0:T(8,128)(2,1)} %copy-done.4) | copy-start | bytes 1572868
  168.8 17.5 %all-to-all-start.2 = ((bf16[4,128,512]{2,1,0:T(8,128)(2,1)}), bf16[4,128,512]{2,1,0:T(8,128)(2,1)S(1)}, u32[]{:S(2)}, u32[]{:S(2)}) async-start(bf16[4,128,512]{2,1,0:T(8,128)(2,1)} %convert_element_type.107), calls=%async_computation.2 | async-start | bytes 1048576 | tf_op jit(solution)/shard_map/all_to_all | solution.py:149
  172.2 1.0 copy-start.6
  175.4 10.9 %collective-permute-start.3 = (bf16[128,512]{1,0:T(8,128)(2,1)S(1)}, bf16[128,512]{1,0:T(8,128)(2,1)S(1)}, u32[]{:S(2)}, u32[]{:S(2)}) collective-permute-start(bf16[128,512]{1,0:T(8,128)(2,1)S(1)} %reduce_sum.61), channel_id=1, source_target_pairs={{4,0},{8,4},{12,8},{16,12},{20,16},{24,20},{28,24},{5,1},{9,5},{13... | collective-permute-start | bytes 393224 | tf_op jit(solution)/shard_map/ppermute | solution.py:15
  176.8 10.2 %collective-permute-start.4 = (bf16[128,512]{1,0:T(8,128)(2,1)S(1)}, bf16[128,512]{1,0:T(8,128)(2,1)S(1)}, u32[]{:S(2)}, u32[]{:S(2)}) collective-permute-start(bf16[128,512]{1,0:T(8,128)(2,1)S(1)} %reduce_sum.63), channel_id=1, source_target_pairs={{4,0},{8,4},{12,8},{16,12},{20,16},{24,20},{28,24},{5,1},{9,5},{13... | collective-permute-start | bytes 393224 | tf_op jit(solution)/shard_map/ppermute | solution.py:15
where the time goes:
time: 189 us; the launch traced here: 188 us
  blocking collectives  45.2 us (24%)
  waiting for transfers between devices  44.8 us (24%)
  matrix products  25.4 us (13%)
  starting transfers between devices  24.1 us (13%)
  other arithmetic  23.8 us (13%)
  local copies, waits for them, and re-layouts  22.5 us (12%)
    all_gather x1, blocking collectives, body(): lax.all_gather(keys, 'grp', axis=0, tiled=True)  17.7 us
    all_gather x1, blocking collectives, body(): lax.all_gather(values, 'grp', axis=0, tiled=True)  17.2 us
    all_to_all x1, waiting for transfers between devices, body(): lax.all_to_all(far_dkeys.astype(jnp.bfloat16), 'grp', split_axis=0, conca...  13.4 us
    all_to_all x1, waiting for transfers between devices, body(): lax.all_to_all(far_dvalues.astype(jnp.bfloat16), 'grp', split_axis=0, con...  12.4 us
    all_to_all x1, waiting for transfers between devices, body(): lax.all_to_all(near_dkeys.astype(jnp.bfloat16), 'grp', split_axis=0, conc...  12 us
    all_gather x1, blocking collectives, body(): lax.all_gather(segments, 'grp', axis=0, tiled=True)  10.2 us
    ppermute x5, starting transfers between devices, from_behind(): lax.ppermute(value, axis, [(source, source + steps) for source in range(i...  8.9 us
    all_to_all x1, waiting for transfers between devices, body(): lax.all_to_all(near_dvalues.astype(jnp.bfloat16), 'grp', split_axis=0, co...  6.99 us
  transfers between devices with their start and end apart: 9, of which 4 were waited for; matrix products, arithmetic and copies ran while one was open for 10% of the time, Pallas kernels for 0%

commit v1 on v0

v1 whole, which is shorter than its diff:
```python
import functools

import jax
import jax.numpy as jnp
from jax import lax
from jax.experimental import pallas as pl
from jax.experimental.pallas import tpu as pltpu
from jax.sharding import PartitionSpec as P


KV_HEADS = 4
CHUNKS = 1
SEG_ROWS = 8
NEG = -1e30
LOG2E = 1.4426950408889634

VMEM = pl.BlockSpec(memory_space=pltpu.VMEM)
SMEM = pl.BlockSpec(memory_space=pltpu.SMEM)
HBM = pl.BlockSpec(memory_space=pltpu.HBM)
F32 = jnp.float32
BF16 = jnp.bfloat16


def nbytes(*arrays):
    return sum(a.size * a.dtype.itemsize for a in arrays)


def call(kernel, outs, ins, in_specs, scratch=(), flops=0):
    cost = pl.CostEstimate(flops=flops, bytes_accessed=nbytes(*ins, *outs), transcendentals=0)
    return pl.pallas_call(
        kernel,
        out_shape=outs,
        in_specs=in_specs,
        out_specs=[VMEM] * len(outs),
        scratch_shapes=list(scratch),
        cost_estimate=cost,
        compiler_params=pltpu.CompilerParams(vmem_limit_bytes=32 * 1024 * 1024),
    )(*ins)


def pack_kernel(chunks, k_ref, v_ref, s_ref, *refs):
    outs, (seg, sems) = refs[:chunks], refs[chunks:]
    tile, kv = k_ref.shape
    part = kv // chunks
    copies = [pltpu.make_async_copy(s_ref, seg, sems.at[2 * chunks])]
    for i, out in enumerate(outs):
        cols = pl.ds(i * part, part)
        for j, ref in enumerate((k_ref, v_ref)):
            target = out.at[pl.ds(0, tile), pl.ds(j * part, part)]
            copies.append(pltpu.make_async_copy(ref.at[:, cols], target, sems.at[2 * i + j]))
    for copy in copies:
        copy.start()
    copies[0].wait()
    for out in outs:
        out[tile:, :] = jnp.zeros((SEG_ROWS, 2 * part), BF16)
        out[tile:, 0:tile] = jnp.broadcast_to(seg[...].astype(F32), (SEG_ROWS, tile)).astype(BF16)
    for copy in copies[1:]:
        copy.wait()


def attend_kernel(heads, group, ids_ref, count_ref, q_ref, g_ref, s_ref, *refs):
    tiles = 2 * group
    pool = refs[:tiles]
    att_ref, gq_ref = refs[tiles : tiles + 2]
    near = refs[tiles + 2 : tiles + 2 + group]
    far = refs[tiles + 2 + group : tiles + 2 + tiles]
    kv_s, seg_s, bias_s, term_s = refs[tiles + 2 + tiles :]
    tile = q_ref.shape[0]
    width = kv_s.shape[1]
    half = width // 2
    size = half // heads
    slots = ids_ref.shape[1]
    per = q_ref.shape[1] // half
    scaling = size ** (-0.5)

    me = lax.axis_index("grp")
    first = (lax.axis_index("cp") - 1) * group
    count = count_ref[0]

    def slot_of(place):
        steps, is_far = place % group, place >= group
        row = lax.rem(me - steps + group, group)
        want = first + row + (0 if is_far else group)
        found = jnp.int32(-1)
        for j in range(slots):
            found = jnp.where((ids_ref[0, j] == want) & (j < count), j, found)
        return found

    slot = [slot_of(p) for p in range(tiles)]
    for j in range(1, slots):

        @pl.when(j >= count)
        def _():
            kv_s[j * tile : (j + 1) * tile, :] = jnp.zeros((tile, width), BF16)
            seg_s[j] = jnp.full((SEG_ROWS, tile), -1.0, F32)

    for p in range(tiles):

        @pl.when(slot[p] >= 0)
        def _():
            start = pl.multiple_of(slot[p] * tile, tile)
            kv_s[pl.ds(start, tile), :] = pool[p][0:tile, :]
            seg_s[slot[p]] = pool[p][tile:, 0:tile].astype(F32)

    own = jnp.broadcast_to(s_ref[...].astype(F32), (tile, tile)).T
    for j in range(slots):
        bias_s[:, j * tile : (j + 1) * tile] = jnp.where(own == seg_s[j][0:1, :], 0.0, NEG)

    nt = (((1,), (1,)), ((), ()))
    for h in range(heads):
        k = kv_s[:, h * size : (h + 1) * size]
        v = kv_s[:, half + h * size : half + (h + 1) * size]
        span = range(h * per, (h + 1) * per)
        qs = jnp.concatenate([q_ref[:, x * size : (x + 1) * size] for x in span], axis=0)
        gs = jnp.concatenate([g_ref[:, x * size : (x + 1) * size] for x in span], axis=0)
        s = lax.dot_general(qs, k, nt, preferred_element_type=F32)
        dp = lax.dot_general(gs, v, nt, preferred_element_type=F32)
        bias = jnp.concatenate([bias_s[...]] * per, axis=0)
        s = s * (scaling * LOG2E) + bias
        e = jnp.exp2(s - jnp.max(s, axis=1, keepdims=True))
        p = e * (1.0 / jnp.sum(e, axis=1, keepdims=True))
        w = p.astype(BF16)
        a = jnp.dot(w, v, preferred_element_type=F32).astype(BF16)
        delta = jnp.sum(a.astype(F32) * gs.astype(F32), axis=1, keepdims=True)
        ds = (p * (dp - delta)).astype(BF16)
        gq = (jnp.dot(ds, k, preferred_element_type=F32) * scaling).astype(BF16)
        for i, x in enumerate(span):
            att_ref[:, x * size : (x + 1) * size] = a[i * tile : (i + 1) * tile]
            gq_ref[:, x * size : (x + 1) * size] = gq[i * tile : (i + 1) * tile]
        dk = jnp.dot(qs.T, ds, preferred_element_type=F32)
        term_s[:, h * size : (h + 1) * size] = (dk * scaling).T.astype(BF16)
        dv = jnp.dot(gs.T, w, preferred_element_type=F32)
        term_s[:, half + h * size : half + (h + 1) * size] = dv.T.astype(BF16)

    for p in range(tiles):
        out = near[p] if p < group else far[p - group]

        @pl.when(slot[p] >= 0)
        def _():
            out[...] = term_s[pl.ds(pl.multiple_of(slot[p] * tile, tile), tile), :]

        @pl.when(slot[p] < 0)
        def _():
            out[...] = jnp.zeros(out.shape, BF16)


def join_kernel(near, far, out):
    out[...] = (near[...].astype(F32) + far[...].astype(F32)).astype(out.dtype)


def total_kernel(chunks, parts, *refs):
    ins, (k_ref, v_ref) = refs[: chunks * parts], refs[chunks * parts :]
    part = k_ref.shape[1] // chunks
    for i in range(chunks):
        total = ins[i * parts][...]
        for one in ins[i * parts + 1 : (i + 1) * parts]:
            total += one[...].astype(F32)
        k_ref[:, i * part : (i + 1) * part] = total[:, :part].astype(BF16)
        v_ref[:, i * part : (i + 1) * part] = total[:, part:].astype(BF16)


def rotate(x, steps):
    count = lax.axis_size("grp")
    return lax.ppermute(x, "grp", [(i, (i + steps) % count) for i in range(count)])


def shift(x, steps):
    count = lax.axis_size("cp")
    return lax.ppermute(x, "cp", [(i, i + steps) for i in range(count) if 0 <= i + steps < count])


def near_first(group):
    order = []
    for d in range(1, group // 2 + 1):
        order += [d] if 2 * d == group else [d, group - d]
    return order


def body(queries, keys, values, grad_out, segments, block_ids, block_count):
    tile, kv = keys.shape
    full = queries.shape[1]
    group = lax.axis_size("grp")
    slots = block_ids.shape[1]
    heads = KV_HEADS // CHUNKS
    part = kv // CHUNKS
    width = 2 * part
    qpart = full // CHUNKS
    order = near_first(group)
    seg = segments.reshape(1, tile)
    payload = jax.ShapeDtypeStruct((tile + SEG_ROWS, width), BF16)
    packed = call(
        functools.partial(pack_kernel, CHUNKS),
        [payload] * CHUNKS,
        [keys, values, seg],
        [HBM] * 3,
        scratch=[pltpu.VMEM((1, tile), jnp.int32), pltpu.SemaphoreType.DMA((2 * CHUNKS + 1,))],
    )
    q_out = jax.ShapeDtypeStruct((tile, qpart), BF16)
    term = jax.ShapeDtypeStruct((tile, width), BF16)
    kept = jax.ShapeDtypeStruct((tile, width), F32)
    sums, att, gq = [], [], []
    for i in range(CHUNKS):
        near, far = [packed[i]] * group, [None] * group
        for d in order:
            near[d] = rotate(packed[i], d)
        for d in [0] + order:
            far[d] = shift(near[d], 1)
        cols = slice(i * qpart, (i + 1) * qpart)
        outs = call(
            functools.partial(attend_kernel, heads, group),
            [q_out, q_out] + [term] * (2 * group),
            [block_ids, block_count, queries[:, cols], grad_out[:, cols], seg, *near, *far],
            [SMEM, SMEM] + [VMEM] * (3 + 2 * group),
            scratch=[
                pltpu.VMEM((slots * tile, width), BF16),
                pltpu.VMEM((slots, SEG_ROWS, tile), F32),
                pltpu.VMEM((tile, slots * tile), F32),
                pltpu.VMEM((slots * tile, width), BF16),
            ],
            flops=12 * tile * slots * tile * qpart,
        )
        att.append(outs[0])
        gq.append(outs[1])
        near_terms, far_terms = outs[2 : 2 + group], outs[2 + group :]
        mine = [None] * group
        for d in order + [0]:
            later = shift(far_terms[d], -1)
            mine[d] = call(
                join_kernel, [term if d else kept], [near_terms[d], later], [VMEM] * 2
            )[0]
            if d:
                mine[d] = rotate(mine[d], -d)
        sums += mine
    dk, dv = call(
        functools.partial(total_kernel, CHUNKS, group),
        [jax.ShapeDtypeStruct((tile, kv), BF16)] * 2,
        sums,
        [VMEM] * len(sums),
    )
    if CHUNKS == 1:
        return att[0], gq[0], dk, dv
    return jnp.concatenate(att, axis=1), jnp.concatenate(gq, axis=1), dk, dv


def solution(mesh):
    two, one = P(("cp", "grp"), None), P(("cp", "grp"))
    return jax.shard_map(
        body,
        mesh=mesh,
        in_specs=(two, two, two, two, one, two, one),
        out_specs=(two,) * 4,
        check_vma=False,
    )
```

time: 189 us -> 84.2 us (0.45)
  the two profiles are of different devices: /device:TPU:0 before, /device:TPU:21 now
where the time goes in v1:
time: 84.2 us; the launch traced here: 83.8 us
  waiting for transfers between devices  36.2 us (43%)
  starting transfers between devices  34.8 us (41%)
  Pallas kernels  7.83 us (9%)
  local copies, waits for them, and re-layouts  3.51 us (4%)
  between operations  1.44 us (2%)
    ppermute x6, waiting for transfers between devices, rotate(): lax.ppermute(x, 'grp', [(i, (i + steps) % count) for i in range(count)])  29.6 us
    ppermute x8, starting transfers between devices, shift(): lax.ppermute(x, 'cp', [(i, i + steps) for i in range(count) if 0 <= i + s...  28.1 us
    pallas_call x7, Pallas kernels, call(): pl.pallas_call(kernel, out_shape=outs, in_specs=in_specs, out_specs=[VMEM...  7.83 us
    ppermute x6, starting transfers between devices, rotate(): lax.ppermute(x, 'grp', [(i, (i + steps) % count) for i in range(count)])  6.7 us
    ppermute x8, waiting for transfers between devices, shift(): lax.ppermute(x, 'cp', [(i, i + steps) for i in range(count) if 0 <= i + s...  6.54 us
    unnamed x12, local copies, waits for them, and re-layouts  3.51 us
  transfers between devices with their start and end apart: 14, of which 8 were waited for; matrix products, arithmetic and copies ran while one was open for 0% of the time, Pallas kernels for 0%

profile of v1, /device:TPU:21, one launch (start us, length us, event | category | flops | bytes accessed | tf_op | source)
XLA Modules:
  0.0 83.8 jit_solution(3663073980270354542)
XLA Ops:
  0.6 0.6 copy-done.2
  1.3 0.9 %copy-done = bf16[128,512]{1,0:T(8,128)(2,1)S(1)} copy-done((bf16[128,512]{1,0:T(8,128)(2,1)S(1)}, bf16[128,512]{1,0:T(8,128)(2,1)}, u32[]{:S(2)}) %copy-start) | copy-done | bytes 131096
  2.2 0.9 %copy-done.1 = bf16[128,512]{1,0:T(8,128)(2,1)S(1)} copy-done((bf16[128,512]{1,0:T(8,128)(2,1)S(1)}, bf16[128,512]{1,0:T(8,128)(2,1)}, u32[]{:S(2)}) %copy-start.1) | copy-done | bytes 131096
  3.1 0.1 shard_map.102.refs_0_
  3.2 0.2 collective-permute-start.2
  3.4 3.2 %collective-permute-start.1 = (bf16[136,1024]{1,0:T(8,128)(2,1)S(1)}, bf16[136,1024]{1,0:T(8,128)(2,1)S(1)}, u32[]{:S(2)}, u32[]{:S(2)}) collective-permute-start(bf16[136,1024]{1,0:T(8,128)(2,1)S(1)} %shard_map.102.refs_0_), channel_id=1, source_target_pairs={{0,2},{1,3},{2,0},{3,1},{4,6},{5,7},{6,4},{7,5},{8,10},{9,11},{10,... | collective-permute-start | bytes 835592 | tf_op jit(solution)/shard_map/ppermute | solution.py:164
  6.6 4.2 %collective-permute-start.3 = (bf16[136,1024]{1,0:T(8,128)(2,1)S(1)}, bf16[136,1024]{1,0:T(8,128)(2,1)S(1)}, u32[]{:S(2)}, u32[]{:S(2)}) collective-permute-start(bf16[136,1024]{1,0:T(8,128)(2,1)S(1)} %shard_map.102.refs_0_), channel_id=1, source_target_pairs={{0,4},{4,8},{8,12},{12,16},{16,20},{20,24},{24,28},{1,5},{5,9},{9,... | collective-permute-start | bytes 835592 | tf_op jit(solution)/shard_map/ppermute | solution.py:169
  10.9 5.6 %collective-permute-start.6 = (bf16[136,1024]{1,0:T(8,128)(2,1)S(1)}, bf16[136,1024]{1,0:T(8,128)(2,1)S(1)}, u32[]{:S(2)}, u32[]{:S(2)}) collective-permute-start(bf16[136,1024]{1,0:T(8,128)(2,1)S(1)} %collective-permute-done.2.refs_3_), channel_id=1, source_target_pairs={{0,4},{4,8},{8,12},{12,16},{16,20},{20,24},{24,28},{1,5},{5,9},{9,... | collective-permute-start | bytes 835592 | tf_op jit(solution)/shard_map/ppermute | solution.py:169
  16.4 10.2 %collective-permute-done.1.refs_2_ = bf16[136,1024]{1,0:T(8,128)(2,1)S(1)} collective-permute-done((bf16[136,1024]{1,0:T(8,128)(2,1)S(1)}, bf16[136,1024]{1,0:T(8,128)(2,1)S(1)}, u32[]{:S(2)}, u32[]{:S(2)}) %collective-permute-start.1) | collective-permute-done | bytes 278560 | tf_op jit(solution)/shard_map/ppermute | solution.py:164
  26.7 4.5 %collective-permute-start.5 = (bf16[136,1024]{1,0:T(8,128)(2,1)S(1)}, bf16[136,1024]{1,0:T(8,128)(2,1)S(1)}, u32[]{:S(2)}, u32[]{:S(2)}) collective-permute-start(bf16[136,1024]{1,0:T(8,128)(2,1)S(1)} %collective-permute-done.1.refs_2_), channel_id=1, source_target_pairs={{0,4},{4,8},{8,12},{12,16},{16,20},{20,24},{24,28},{1,5},{5,9},{9,... | collective-permute-start | bytes 835592 | tf_op jit(solution)/shard_map/ppermute | solution.py:169
  31.2 3.2 %collective-permute-start.4 = (bf16[136,1024]{1,0:T(8,128)(2,1)S(1)}, bf16[136,1024]{1,0:T(8,128)(2,1)S(1)}, u32[]{:S(2)}, u32[]{:S(2)}) collective-permute-start(bf16[136,1024]{1,0:T(8,128)(2,1)S(1)} %collective-permute-done.refs_1_), channel_id=1, source_target_pairs={{0,4},{4,8},{8,12},{12,16},{16,20},{20,24},{24,28},{1,5},{5,9},{9,... | collective-permute-start | bytes 835592 | tf_op jit(solution)/shard_map/ppermute | solution.py:169
  35.1 2.8 %collective-permute-done.4.refs_5_ = bf16[136,1024]{1,0:T(8,128)(2,1)S(1)} collective-permute-done((bf16[136,1024]{1,0:T(8,128)(2,1)S(1)}, bf16[136,1024]{1,0:T(8,128)(2,1)S(1)}, u32[]{:S(2)}, u32[]{:S(2)}) %collective-permute-start.4) | collective-permute-done | bytes 278560 | tf_op jit(solution)/shard_map/ppermute | solution.py:169
  37.9 1.0 %copy-done.4 = bf16[128,2048]{1,0:T(8,128)(2,1)S(1)} copy-done((bf16[128,2048]{1,0:T(8,128)(2,1)S(1)}, bf16[128,2048]{1,0:T(8,128)(2,1)}, u32[]{:S(2)}) %copy-start.4) | copy-done | bytes 524312
  39.0 6.7 %shard_map.103 = (bf16[128,2048]{1,0:T(8,128)(2,1)}, bf16[128,2048]{1,0:T(8,128)(2,1)}, bf16[128,1024]{1,0:T(8,128)(2,1)S(1)}, bf16[128,1024]{1,0:T(8,128)(2,1)S...) custom-call(s32[1,4]{1,0:T(1,128)S(1)} %copy-done.5, ...), custom_call_target="tpu_custom_call" | custom-call | flops 1610612736 | bytes 6423060 | tf_op jit(solution)/shard_map/pallas_call | solution.py:30
  45.7 4.2 %collective-permute-start.8 = (bf16[128,1024]{1,0:T(8,128)(2,1)S(1)}, bf16[128,1024]{1,0:T(8,128)(2,1)S(1)}, u32[]{:S(2)}, u32[]{:S(2)}) collective-permute-start(bf16[128,1024]{1,0:T(8,128)(2,1)S(1)} %get-tuple-element.21), channel_id=1, source_target_pairs={{4,0},{8,4},{12,8},{16,12},{20,16},{24,20},{28,24},{5,1},{9,5},{13... | collective-permute-start | bytes 786440 | tf_op jit(solution)/shard_map/ppermute | solution.py:169
  49.9 1.9 %collective-permute-start.10 = (bf16[128,1024]{1,0:T(8,128)(2,1)S(1)}, bf16[128,1024]{1,0:T(8,128)(2,1)S(1)}, u32[]{:S(2)}, u32[]{:S(2)}) collective-permute-start(bf16[128,1024]{1,0:T(8,128)(2,1)S(1)} %get-tuple-element.23), channel_id=1, source_target_pairs={{4,0},{8,4},{12,8},{16,12},{20,16},{24,20},{28,24},{5,1},{9,5},{13... | collective-permute-start | bytes 786440 | tf_op jit(solution)/shard_map/ppermute | solution.py:169
  51.8 2.5 %collective-permute-start.12 = (bf16[128,1024]{1,0:T(8,128)(2,1)S(1)}, bf16[128,1024]{1,0:T(8,128)(2,1)S(1)}, u32[]{:S(2)}, u32[]{:S(2)}) collective-permute-start(bf16[128,1024]{1,0:T(8,128)(2,1)S(1)} %get-tuple-element.25), channel_id=1, source_target_pairs={{4,0},{8,4},{12,8},{16,12},{20,16},{24,20},{28,24},{5,1},{9,5},{13... | collective-permute-start | bytes 786440 | tf_op jit(solution)/shard_map/ppermute | solution.py:169
  54.4 1.9 %collective-permute-start.7 = (bf16[128,1024]{1,0:T(8,128)(2,1)S(1)}, bf16[128,1024]{1,0:T(8,128)(2,1)S(1)}, u32[]{:S(2)}, u32[]{:S(2)}) collective-permute-start(bf16[128,1024]{1,0:T(8,128)(2,1)S(1)} %get-tuple-element.19), channel_id=1, source_target_pairs={{4,0},{8,4},{12,8},{16,12},{20,16},{24,20},{28,24},{5,1},{9,5},{13... | collective-permute-start | bytes 786440 | tf_op jit(solution)/shard_map/ppermute | solution.py:169
  56.3 0.1 shard_map.105
  56.4 0.2 collective-permute-start.9
  56.5 1.1 %collective-permute-done.10.far = bf16[128,1024]{1,0:T(8,128)(2,1)S(1)} collective-permute-done((bf16[128,1024]{1,0:T(8,128)(2,1)S(1)}, bf16[128,1024]{1,0:T(8,128)(2,1)S(1)}, u32[]{:S(2)}, u32[]{:S(2)}) %collective-permute-start.10) | collective-permute-done | bytes 262176 | tf_op jit(solution)/shard_map/ppermute | solution.py:169
  57.6 0.1 shard_map.106
  57.7 2.9 %collective-permute-start.11 = (bf16[128,1024]{1,0:T(8,128)(2,1)S(1)}, bf16[128,1024]{1,0:T(8,128)(2,1)S(1)}, u32[]{:S(2)}, u32[]{:S(2)}) collective-permute-start(bf16[128,1024]{1,0:T(8,128)(2,1)S(1)} %shard_map.106), channel_id=1, source_target_pairs={{0,2},{1,3},{2,0},{3,1},{4,6},{5,7},{6,4},{7,5},{8,10},{9,11},{10,... | collective-permute-start | bytes 786440 | tf_op jit(solution)/shard_map/ppermute | solution.py:164
  60.6 0.1 collective-permute-done.12.far
  60.7 0.1 shard_map.107
  60.8 0.2 collective-permute-start.13
  61.0 2.5 %collective-permute-done.7.far = bf16[128,1024]{1,0:T(8,128)(2,1)S(1)} collective-permute-done((bf16[128,1024]{1,0:T(8,128)(2,1)S(1)}, bf16[128,1024]{1,0:T(8,128)(2,1)S(1)}, u32[]{:S(2)}, u32[]{:S(2)}) %collective-permute-start.7) | collective-permute-done | bytes 262176 | tf_op jit(solution)/shard_map/ppermute | solution.py:169
  63.5 0.1 shard_map.104.refs_0_
  63.6 0.7 collective-permute-done.9.refs_1_
  64.3 14.8 %collective-permute-done.11.refs_2_ = bf16[128,1024]{1,0:T(8,128)(2,1)S(1)} collective-permute-done((bf16[128,1024]{1,0:T(8,128)(2,1)S(1)}, bf16[128,1024]{1,0:T(8,128)(2,1)S(1)}, u32[]{:S(2)}, u32[]{:S(2)}) %collective-permute-start.11) | collective-permute-done | bytes 262176 | tf_op jit(solution)/shard_map/ppermute | solution.py:164
  79.0 4.0 %collective-permute-done.13.refs_3_ = bf16[128,1024]{1,0:T(8,128)(2,1)S(1)} collective-permute-done((bf16[128,1024]{1,0:T(8,128)(2,1)S(1)}, bf16[128,1024]{1,0:T(8,128)(2,1)S(1)}, u32[]{:S(2)}, u32[]{:S(2)}) %collective-permute-start.13) | collective-permute-done | bytes 262176 | tf_op jit(solution)/shard_map/ppermute | solution.py:164
  83.0 0.8 shard_map.108
  (15 shorter events, 0.0 us)
Async XLA Ops:
  0.6 0.7 copy-start.2
  1.3 0.9 %copy-start = (bf16[128,512]{1,0:T(8,128)(2,1)S(1)}, bf16[128,512]{1,0:T(8,128)(2,1)}, u32[]{:S(2)}) copy-start(bf16[128,512]{1,0:T(8,128)(2,1)} %k_ref.1) | copy-start | bytes 393220
  2.2 0.9 %copy-start.1 = (bf16[128,512]{1,0:T(8,128)(2,1)S(1)}, bf16[128,512]{1,0:T(8,128)(2,1)}, u32[]{:S(2)}) copy-start(bf16[128,512]{1,0:T(8,128)(2,1)} %v_ref.1) | copy-start | bytes 393220
  3.1 34.8 %copy-start.3 = (bf16[128,2048]{1,0:T(8,128)(2,1)S(1)}, bf16[128,2048]{1,0:T(8,128)(2,1)}, u32[]{:S(2)}) copy-start(bf16[128,2048]{1,0:T(8,128)(2,1)} %q_ref.1) | copy-start | bytes 1572868
  3.2 34.7 %copy-start.5 = (s32[1,4]{1,0:T(1,128)S(1)}, s32[1,4]{1,0:T(1,128)}, u32[]{:S(2)}) copy-start(s32[1,4]{1,0:T(1,128)} %ids_ref.1) | copy-start | bytes 52
  3.2 7.7 %collective-permute-start.2 = (bf16[136,1024]{1,0:T(8,128)(2,1)S(1)}, bf16[136,1024]{1,0:T(8,128)(2,1)S(1)}, u32[]{:S(2)}, u32[]{:S(2)}) collective-permute-start(bf16[136,1024]{1,0:T(8,128)(2,1)S(1)} %shard_map.102.refs_0_), channel_id=1, source_target_pairs={{0,3},{1,0},{2,1},{3,2},{4,7},{5,4},{6,5},{7,6},{8,11},{9,8},{10,9... | collective-permute-start | bytes 835592 | tf_op jit(solution)/shard_map/ppermute | solution.py:164
  3.4 23.2 %collective-permute-start.1 = (bf16[136,1024]{1,0:T(8,128)(2,1)S(1)}, bf16[136,1024]{1,0:T(8,128)(2,1)S(1)}, u32[]{:S(2)}, u32[]{:S(2)}) collective-permute-start(bf16[136,1024]{1,0:T(8,128)(2,1)S(1)} %shard_map.102.refs_0_), channel_id=1, source_target_pairs={{0,2},{1,3},{2,0},{3,1},{4,6},{5,7},{6,4},{7,5},{8,10},{9,11},{10,... | collective-permute-start | bytes 835592 | tf_op jit(solution)/shard_map/ppermute | solution.py:164
  6.6 24.6 %collective-permute-start = (bf16[136,1024]{1,0:T(8,128)(2,1)S(1)}, bf16[136,1024]{1,0:T(8,128)(2,1)S(1)}, u32[]{:S(2)}, u32[]{:S(2)}) collective-permute-start(bf16[136,1024]{1,0:T(8,128)(2,1)S(1)} %shard_map.102.refs_0_), channel_id=1, source_target_pairs={{0,1},{1,2},{2,3},{3,0},{4,5},{5,6},{6,7},{7,4},{8,9},{9,10},{10,1... | collective-permute-start | bytes 835592 | tf_op jit(solution)/shard_map/ppermute | solution.py:164
  6.6 28.5 %collective-permute-start.3 = (bf16[136,1024]{1,0:T(8,128)(2,1)S(1)}, bf16[136,1024]{1,0:T(8,128)(2,1)S(1)}, u32[]{:S(2)}, u32[]{:S(2)}) collective-permute-start(bf16[136,1024]{1,0:T(8,128)(2,1)S(1)} %shard_map.102.refs_0_), channel_id=1, source_target_pairs={{0,4},{4,8},{8,12},{12,16},{16,20},{20,24},{24,28},{1,5},{5,9},{9,... | collective-permute-start | bytes 835592 | tf_op jit(solution)/shard_map/ppermute | solution.py:169
  10.9 24.2 %collective-permute-start.6 = (bf16[136,1024]{1,0:T(8,128)(2,1)S(1)}, bf16[136,1024]{1,0:T(8,128)(2,1)S(1)}, u32[]{:S(2)}, u32[]{:S(2)}) collective-permute-start(bf16[136,1024]{1,0:T(8,128)(2,1)S(1)} %collective-permute-done.2.refs_3_), channel_id=1, source_target_pairs={{0,4},{4,8},{8,12},{12,16},{16,20},{20,24},{24,28},{1,5},{5,9},{9,... | collective-permute-start | bytes 835592 | tf_op jit(solution)/shard_map/ppermute | solution.py:169
  26.7 8.5 %collective-permute-start.5 = (bf16[136,1024]{1,0:T(8,128)(2,1)S(1)}, bf16[136,1024]{1,0:T(8,128)(2,1)S(1)}, u32[]{:S(2)}, u32[]{:S(2)}) collective-permute-start(bf16[136,1024]{1,0:T(8,128)(2,1)S(1)} %collective-permute-done.1.refs_2_), channel_id=1, source_target_pairs={{0,4},{4,8},{8,12},{12,16},{16,20},{20,24},{24,28},{1,5},{5,9},{9,... | collective-permute-start | bytes 835592 | tf_op jit(solution)/shard_map/ppermute | solution.py:169
  31.2 6.7 %collective-permute-start.4 = (bf16[136,1024]{1,0:T(8,128)(2,1)S(1)}, bf16[136,1024]{1,0:T(8,128)(2,1)S(1)}, u32[]{:S(2)}, u32[]{:S(2)}) collective-permute-start(bf16[136,1024]{1,0:T(8,128)(2,1)S(1)} %collective-permute-done.refs_1_), channel_id=1, source_target_pairs={{0,4},{4,8},{8,12},{12,16},{16,20},{20,24},{24,28},{1,5},{5,9},{9,... | collective-permute-start | bytes 835592 | tf_op jit(solution)/shard_map/ppermute | solution.py:169
  37.9 1.0 %copy-start.4 = (bf16[128,2048]{1,0:T(8,128)(2,1)S(1)}, bf16[128,2048]{1,0:T(8,128)(2,1)}, u32[]{:S(2)}) copy-start(bf16[128,2048]{1,0:T(8,128)(2,1)} %g_ref.1) | copy-start | bytes 1572868
  45.7 10.6 %collective-permute-start.8 = (bf16[128,1024]{1,0:T(8,128)(2,1)S(1)}, bf16[128,1024]{1,0:T(8,128)(2,1)S(1)}, u32[]{:S(2)}, u32[]{:S(2)}) collective-permute-start(bf16[128,1024]{1,0:T(8,128)(2,1)S(1)} %get-tuple-element.21), channel_id=1, source_target_pairs={{4,0},{8,4},{12,8},{16,12},{20,16},{24,20},{28,24},{5,1},{9,5},{13... | collective-permute-start | bytes 786440 | tf_op jit(solution)/shard_map/ppermute | solution.py:169
  49.9 7.7 %collective-permute-start.10 = (bf16[128,1024]{1,0:T(8,128)(2,1)S(1)}, bf16[128,1024]{1,0:T(8,128)(2,1)S(1)}, u32[]{:S(2)}, u32[]{:S(2)}) collective-permute-start(bf16[128,1024]{1,0:T(8,128)(2,1)S(1)} %get-tuple-element.23), channel_id=1, source_target_pairs={{4,0},{8,4},{12,8},{16,12},{20,16},{24,20},{28,24},{5,1},{9,5},{13... | collective-permute-start | bytes 786440 | tf_op jit(solution)/shard_map/ppermute | solution.py:169
  51.8 8.9 %collective-permute-start.12 = (bf16[128,1024]{1,0:T(8,128)(2,1)S(1)}, bf16[128,1024]{1,0:T(8,128)(2,1)S(1)}, u32[]{:S(2)}, u32[]{:S(2)}) collective-permute-start(bf16[128,1024]{1,0:T(8,128)(2,1)S(1)} %get-tuple-element.25), channel_id=1, source_target_pairs={{4,0},{8,4},{12,8},{16,12},{20,16},{24,20},{28,24},{5,1},{9,5},{13... | collective-permute-start | bytes 786440 | tf_op jit(solution)/shard_map/ppermute | solution.py:169
  54.4 9.1 %collective-permute-start.7 = (bf16[128,1024]{1,0:T(8,128)(2,1)S(1)}, bf16[128,1024]{1,0:T(8,128)(2,1)S(1)}, u32[]{:S(2)}, u32[]{:S(2)}) collective-permute-start(bf16[128,1024]{1,0:T(8,128)(2,1)S(1)} %get-tuple-element.19), channel_id=1, source_target_pairs={{4,0},{8,4},{12,8},{16,12},{20,16},{24,20},{28,24},{5,1},{9,5},{13... | collective-permute-start | bytes 786440 | tf_op jit(solution)/shard_map/ppermute | solution.py:169
  56.4 7.9 %collective-permute-start.9 = (bf16[128,1024]{1,0:T(8,128)(2,1)S(1)}, bf16[128,1024]{1,0:T(8,128)(2,1)S(1)}, u32[]{:S(2)}, u32[]{:S(2)}) collective-permute-start(bf16[128,1024]{1,0:T(8,128)(2,1)S(1)} %shard_map.105), channel_id=1, source_target_pairs={{0,3},{1,0},{2,1},{3,2},{4,7},{5,4},{6,5},{7,6},{8,11},{9,8},{10,9... | collective-permute-start | bytes 786440 | tf_op jit(solution)/shard_map/ppermute | solution.py:164
  57.7 21.4 %collective-permute-start.11 = (bf16[128,1024]{1,0:T(8,128)(2,1)S(1)}, bf16[128,1024]{1,0:T(8,128)(2,1)S(1)}, u32[]{:S(2)}, u32[]{:S(2)}) collective-permute-start(bf16[128,1024]{1,0:T(8,128)(2,1)S(1)} %shard_map.106), channel_id=1, source_target_pairs={{0,2},{1,3},{2,0},{3,1},{4,6},{5,7},{6,4},{7,5},{8,10},{9,11},{10,... | collective-permute-start | bytes 786440 | tf_op jit(solution)/shard_map/ppermute | solution.py:164
  60.8 22.2 %collective-permute-start.13 = (bf16[128,1024]{1,0:T(8,128)(2,1)S(1)}, bf16[128,1024]{1,0:T(8,128)(2,1)S(1)}, u32[]{:S(2)}, u32[]{:S(2)}) collective-permute-start(bf16[128,1024]{1,0:T(8,128)(2,1)S(1)} %shard_map.107), channel_id=1, source_target_pairs={{0,1},{1,2},{2,3},{3,0},{4,5},{5,6},{6,7},{7,4},{8,9},{9,10},{10,1... | collective-permute-start | bytes 786440 | tf_op jit(solution)/shard_map/ppermute | solution.py:164

commit v2 on v1

v2 whole, which is shorter than its diff:
```python
import functools

import jax
import jax.numpy as jnp
from jax import lax
from jax.experimental import pallas as pl
from jax.experimental.pallas import tpu as pltpu
from jax.sharding import PartitionSpec as P


KV_HEADS = 4
PAIR = 2
BLOCK_ROWS = 64
NEG = -1e30
LOG2E = 1.4426950408889634

VMEM = pl.BlockSpec(memory_space=pltpu.VMEM)
SMEM = pl.BlockSpec(memory_space=pltpu.SMEM)
F32 = jnp.float32
BF16 = jnp.bfloat16


def call(kernel, outs, ins, in_specs=None, scratch=(), flops=0):
    bytes_accessed = sum(a.size * a.dtype.itemsize for a in [*ins, *outs])
    return pl.pallas_call(
        kernel,
        out_shape=outs,
        in_specs=in_specs or [VMEM] * len(ins),
        out_specs=[VMEM] * len(outs),
        scratch_shapes=list(scratch),
        cost_estimate=pl.CostEstimate(
            flops=flops, bytes_accessed=bytes_accessed, transcendentals=0
        ),
        compiler_params=pltpu.CompilerParams(vmem_limit_bytes=32 * 1024 * 1024),
    )(*ins)


def parity():
    return lax.rem(lax.axis_index("grp"), PAIR)


def part_of(index, width):
    return pl.ds(pl.multiple_of(index * width, width), width)


def pack_kernel(group, ids_ref, count_ref, k_ref, v_ref, s_ref, mine_ref, other_ref):
    tile, kv = k_ref.shape
    half = kv // PAIR
    slots = ids_ref.shape[1]
    first = (lax.axis_index("cp") - 1) * group
    notes = [s_ref[...].astype(F32)]
    for j in range(slots):
        notes.append(jnp.full((1, tile), ids_ref[0, j] - first, jnp.int32).astype(F32))
    notes.append(jnp.full((1, tile), count_ref[0], jnp.int32).astype(F32))
    extra = mine_ref.shape[0] - tile
    notes.append(jnp.zeros((extra - len(notes), tile), F32))
    notes = jnp.concatenate(notes, axis=0).astype(BF16)
    for index, out in ((parity(), mine_ref), (1 - parity(), other_ref)):
        out[0:tile, 0:half] = k_ref[:, part_of(index, half)]
        out[0:tile, half:] = v_ref[:, part_of(index, half)]
        out[tile:, :] = jnp.zeros((extra, 2 * half), BF16)
        out[tile:, 0:tile] = notes


def split_kernel(q_ref, g_ref, mine_ref, other_ref):
    tile, full = q_ref.shape
    half = full // PAIR
    size = mine_ref.shape[1]
    for index, out in ((parity(), mine_ref), (1 - parity(), other_ref)):
        for i, ref in enumerate((q_ref, g_ref)):
            for h in range(half // size):
                start = pl.multiple_of(index * half + h * size, size)
                top = (i * (half // size) + h) * tile
                out[top : top + tile, :] = ref[:, pl.ds(start, size)]


def merge_kernel(*refs):
    for i, ref in enumerate(refs[:-1]):
        refs[-1][i] = ref[...]


def attend_kernel(heads, group, partner, qg_ref, *refs):
    pool, far0, farm = refs[:group], refs[group], refs[group + 1]
    refs = refs[group + 2 :]
    if partner:
        before, refs = refs[: group + 1], refs[group + 1 :]
    ag_ref, near, far = refs[0], refs[1 : 1 + group], refs[1 + group]
    kv_s, seg_s, bias_s, term_s, p_s, dp_s, w_s, ds_s = refs[2 + group :]
    slots, width, tile = term_s.shape
    half = width // 2
    size = half // heads
    per = ag_ref.shape[1] // half
    rows = per * tile
    scaling = size ** (-0.5)
    me = lax.axis_index("grp")

    notes = pool[0][tile:, 0:tile]
    if partner:
        notes = jnp.where(parity() == 0, pool[group - 1][tile:, 0:tile], pool[1][tile:, 0:tile])
    notes = notes.astype(F32)
    listed = [jnp.max(notes[1 + j : 2 + j, :]).astype(jnp.int32) for j in range(slots)]
    count = jnp.max(notes[1 + slots : 2 + slots, :]).astype(jnp.int32)

    def slot_of(steps, offset):
        want = lax.rem(me - steps + group, group) + offset
        found = jnp.int32(-1)
        for j in range(slots):
            found = jnp.where((listed[j] == want) & (j < count), j, found)
        return found

    near_slot = [slot_of(d, group) for d in range(group)]
    far_slot = [slot_of(d, 0) for d in range(group)]
    for j in range(1, slots):

        @pl.when(j >= count)
        def _():
            kv_s[j * tile : (j + 1) * tile, :] = jnp.zeros((tile, width), BF16)
            seg_s[j] = jnp.full(seg_s.shape[1:], -1.0, F32)

    far_pool = [far0] + [farm.at[d] for d in range(group - 1)]
    for slot, source in zip(near_slot + far_slot, list(pool) + far_pool):

        @pl.when(slot >= 0)
        def _():
            kv_s[part_of(slot, tile), :] = source[0:tile, :]
            seg_s[slot] = source[tile:, 0:tile].astype(F32)

    own = jnp.broadcast_to(notes[0:1, :], (tile, tile)).T
    for j in range(slots):
        bias_s[:, j * tile : (j + 1) * tile] = jnp.where(own == seg_s[j][0:1, :], 0.0, NEG)

    nt = (((1,), (1,)), ((), ()))
    block = min(BLOCK_ROWS, tile)
    keys_of = lambda h: kv_s[:, h * size : (h + 1) * size]
    values_of = lambda h: kv_s[:, half + h * size : half + (h + 1) * size]
    queries_of = lambda h: qg_ref[h * rows : (h + 1) * rows, :]
    grads_of = lambda h: qg_ref[(heads + h) * rows : (heads + h + 1) * rows, :]

    def products(h):
        p_s[h] = lax.dot_general(queries_of(h), keys_of(h), nt, preferred_element_type=F32)
        dp_s[h] = lax.dot_general(grads_of(h), values_of(h), nt, preferred_element_type=F32)

    def weigh(h):
        for top in range(0, rows, block):
            over = slice(top, top + block)
            s = p_s[h, over, :] * (scaling * LOG2E) + bias_s[top % tile : top % tile + block, :]
            e = jnp.exp2(s - jnp.max(s, axis=1, keepdims=True))
            p = e * (1.0 / jnp.sum(e, axis=1, keepdims=True))
            p_s[h, over, :] = p
            w_s[h, over, :] = p.astype(BF16)

    def finish(h):
        a = jnp.dot(w_s[h], values_of(h), preferred_element_type=F32).astype(BF16)
        delta = jnp.sum(a.astype(F32) * grads_of(h).astype(F32), axis=1, keepdims=True)
        for top in range(0, rows, block):
            over = slice(top, top + block)
            ds = p_s[h, over, :] * (dp_s[h, over, :] - delta[over])
            ds_s[h, over, :] = ds.astype(BF16)
        dv = jnp.dot(grads_of(h).T, w_s[h], preferred_element_type=F32).astype(BF16)
        dk = jnp.dot(queries_of(h).T, ds_s[h], preferred_element_type=F32)
        dk = (dk * scaling).astype(BF16)
        for j in range(slots):
            keys = slice(j * tile, (j + 1) * tile)
            term_s[j, h * size : (h + 1) * size, :] = dk[:, keys]
            term_s[j, half + h * size : half + (h + 1) * size, :] = dv[:, keys]
        gq = (jnp.dot(ds_s[h], keys_of(h), preferred_element_type=F32) * scaling).astype(BF16)
        for i in range(per):
            x = h * per + i
            ag_ref[0:tile, x * size : (x + 1) * size] = a[i * tile : (i + 1) * tile]
            ag_ref[tile:, x * size : (x + 1) * size] = gq[i * tile : (i + 1) * tile]

    products(0)
    for h in range(heads):
        if h + 1 < heads:
            products(h + 1)
        weigh(h)
        finish(h)

    far_out = [far.at[d] for d in range(group)]
    if partner:
        old = list(before[:group]) + [before[group].at[d] for d in range(group)]
    for i, (slot, out) in enumerate(zip(near_slot + far_slot, list(near) + far_out)):

        @pl.when(slot >= 0)
        def _():
            new = term_s[slot].astype(F32)
            out[...] = (new + old[i][...] if partner else new).astype(out.dtype)

        @pl.when(slot < 0)
        def _():
            new = old[i][...] if partner else jnp.zeros((width, tile), F32)
            out[...] = new.astype(out.dtype)


def join_kernel(far, *refs):
    near, outs = refs[: len(refs) // 2], refs[len(refs) // 2 :]
    for d, (one, out) in enumerate(zip(near, outs)):
        out[...] = (one[...] + far[d].astype(F32)).astype(out.dtype)


def total_kernel(group, *refs):
    ins, (k_ref, v_ref) = refs[:group], refs[group:]
    tile, kv = k_ref.shape
    half = kv // PAIR
    for odd in range(PAIR):
        index = parity() if odd == 0 else 1 - parity()
        for top in range(0, half, tile):
            cols = pl.ds(pl.multiple_of(index * half + top, tile), tile)
            for ref, skip in ((k_ref, 0), (v_ref, half)):
                rows = slice(skip + top, skip + top + tile)
                total = ins[odd][rows, :].astype(F32)
                for one in ins[odd + PAIR :: PAIR]:
                    total += one[rows, :].astype(F32)
                ref[:, cols] = total.T.astype(BF16)


def unpack_kernel(mine_ref, other_ref, att_ref, gq_ref):
    tile, full = att_ref.shape
    half = full // PAIR
    for index, ref in ((parity(), mine_ref), (1 - parity(), other_ref)):
        att_ref[:, part_of(index, half)] = ref[0:tile, :]
        gq_ref[:, part_of(index, half)] = ref[tile:, :]


def body(queries, keys, values, grad_out, segments, block_ids, block_count):
    tile, kv = keys.shape
    full = queries.shape[1]
    group, cps = lax.axis_size("grp"), lax.axis_size("cp")
    slots = block_ids.shape[1]
    heads = KV_HEADS // PAIR
    size = kv // KV_HEADS
    width = 2 * kv // PAIR
    per = full // kv
    rows = per * tile
    shape = jax.ShapeDtypeStruct
    ahead = [(i, i + 1) for i in range(cps - 1)]
    back = [(b, a) for a, b in ahead]
    ring = lambda d: [(i, (i + d) % group) for i in range(group)]
    partners = [(i, i + 1 - 2 * (i % PAIR)) for i in range(group)]

    payload = shape((tile + -(-(slots + 2) // 8) * 8, width), BF16)
    mine, other = call(
        functools.partial(pack_kernel, group),
        [payload] * 2,
        [block_ids, block_count, keys, values, segments.reshape(1, tile)],
        in_specs=[SMEM] * 2 + [VMEM] * 3,
    )
    near = [mine]
    for d in range(1, group):
        near.append(lax.ppermute(other if d % PAIR else mine, "grp", ring(d)))
    qg = shape((2 * heads * rows, size), BF16)
    qg_mine, qg_other = call(split_kernel, [qg] * 2, [queries, grad_out])
    qg_partner = lax.ppermute(qg_other, "grp", partners)
    far0 = lax.ppermute(mine, "cp", ahead)
    merged = shape((group - 1, *payload.shape), BF16)
    (merged,) = call(merge_kernel, [merged], near[1:])
    farm = lax.ppermute(merged, "cp", ahead)

    ag = shape((2 * tile, full // PAIR), BF16)
    term = shape((width, tile), F32)
    scratch = [
        pltpu.VMEM((slots * tile, width), BF16),
        pltpu.VMEM((slots, payload.shape[0] - tile, tile), F32),
        pltpu.VMEM((tile, slots * tile), F32),
        pltpu.VMEM((slots, width, tile), BF16),
        pltpu.VMEM((heads, rows, slots * tile), F32),
        pltpu.VMEM((heads, rows, slots * tile), F32),
        pltpu.VMEM((heads, rows, slots * tile), BF16),
        pltpu.VMEM((heads, rows, slots * tile), BF16),
    ]
    flops = 12 * heads * rows * slots * tile * size
    ag_mine, *terms = call(
        functools.partial(attend_kernel, heads, group, False),
        [ag] + [term] * group + [shape((group, width, tile), F32)],
        [qg_mine, *near, far0, farm],
        scratch=scratch,
        flops=flops,
    )
    ag_partner, *terms = call(
        functools.partial(attend_kernel, heads, group, True),
        [ag] + [term] * group + [shape((group, width, tile), BF16)],
        [qg_partner, *near, far0, farm, *terms],
        scratch=scratch,
        flops=flops,
    )
    later = lax.ppermute(terms[group], "cp", back)
    ag_back = lax.ppermute(ag_partner, "grp", partners)
    joined = call(
        join_kernel, [term] + [shape((width, tile), BF16)] * (group - 1), [later, *terms[:group]]
    )
    sums = [joined[0]]
    for d in range(1, group):
        sums.append(lax.ppermute(joined[d], "grp", ring(-d)))
    out = shape((tile, full), BF16)
    attended, grad_queries = call(unpack_kernel, [out] * 2, [ag_mine, ag_back])
    grad = shape((tile, kv), BF16)
    dk, dv = call(functools.partial(total_kernel, group), [grad] * 2, sums)
    return attended, grad_queries, dk, dv


def solution(mesh):
    two, one = P(("cp", "grp"), None), P(("cp", "grp"))
    return jax.shard_map(
        body,
        mesh=mesh,
        in_specs=(two, two, two, two, one, two, one),
        out_specs=(two,) * 4,
        check_vma=False,
    )
```

time: 84.2 us -> 64 us (0.76)
  the two profiles are of different devices: /device:TPU:21 before, /device:TPU:4 now
where the time goes in v2:
time: 64 us; the launch traced here: 63.7 us
  waiting for transfers between devices  30.6 us (48%)
  starting transfers between devices  18.9 us (30%)
  Pallas kernels  8.3 us (13%)
  local copies, waits for them, and re-layouts  4.55 us (7%)
  between operations  1.38 us (2%)
    pallas_call x8, Pallas kernels, call(): pl.pallas_call(kernel, out_shape=outs, in_specs=in_specs or [VMEM] * len(...  8.3 us
    ppermute x1, waiting for transfers between devices, body(): ag_back = lax.ppermute(ag_partner, 'grp', partners)  7.53 us
    ppermute x1, waiting for transfers between devices, body(): later = lax.ppermute(terms[group], 'cp', back)  6.6 us
    ppermute x1, waiting for transfers between devices, body(): far0 = lax.ppermute(mine, 'cp', ahead)  6.31 us
    ppermute x3, waiting for transfers between devices, body(): near.append(lax.ppermute(other if d % PAIR else mine, 'grp', ring(d)))  5.29 us
    ppermute x3, waiting for transfers between devices, body(): sums.append(lax.ppermute(joined[d], 'grp', ring(-d)))  4.83 us
    ppermute x3, starting transfers between devices, body(): near.append(lax.ppermute(other if d % PAIR else mine, 'grp', ring(d)))  4.67 us
    unnamed x12, local copies, waits for them, and re-layouts  4.55 us
  transfers between devices with their start and end apart: 11, of which 7 were waited for; matrix products, arithmetic and copies ran while one was open for 0% of the time, Pallas kernels for 6%

profile of v2, /device:TPU:4, one launch (start us, length us, event | category | flops | bytes accessed | tf_op | source)
XLA Modules:
  0.0 63.7 jit_solution(15164175582356786750)
XLA Ops:
  1.3 0.6 copy-done.4
  1.9 0.0 copy-done.5
  2.0 0.9 %copy-done.2 = bf16[128,512]{1,0:T(8,128)(2,1)S(1)} copy-done((bf16[128,512]{1,0:T(8,128)(2,1)S(1)}, bf16[128,512]{1,0:T(8,128)(2,1)}, u32[]{:S(2)}) %copy-start.2) | copy-done | bytes 131096
  2.9 0.9 %copy-done.3 = bf16[128,512]{1,0:T(8,128)(2,1)S(1)} copy-done((bf16[128,512]{1,0:T(8,128)(2,1)S(1)}, bf16[128,512]{1,0:T(8,128)(2,1)}, u32[]{:S(2)}) %copy-start.3) | copy-done | bytes 131096
  3.8 0.6 shard_map.103
  4.3 3.7 %collective-permute-start.2 = (bf16[136,512]{1,0:T(8,128)(2,1)S(1)}, bf16[136,512]{1,0:T(8,128)(2,1)S(1)}, u32[]{:S(2)}, u32[]{:S(2)}) collective-permute-start(bf16[136,512]{1,0:T(8,128)(2,1)S(1)} %get-tuple-element.30), channel_id=1, source_target_pairs={{0,3},{1,0},{2,1},{3,2},{4,7},{5,4},{6,5},{7,6},{8,11},{9,8},{10,9... | collective-permute-start | bytes 417800 | tf_op jit(solution)/shard_map/ppermute | solution.py:250
  8.0 0.0 collective-permute-start
  8.0 1.0 %collective-permute-start.1 = (bf16[136,512]{1,0:T(8,128)(2,1)S(1)}, bf16[136,512]{1,0:T(8,128)(2,1)S(1)}, u32[]{:S(2)}, u32[]{:S(2)}) collective-permute-start(bf16[136,512]{1,0:T(8,128)(2,1)S(1)} %get-tuple-element.29.refs_0_), channel_id=1, source_target_pairs={{0,2},{1,3},{2,0},{3,1},{4,6},{5,7},{6,4},{7,5},{8,10},{9,11},{10,... | collective-permute-start | bytes 417800 | tf_op jit(solution)/shard_map/ppermute | solution.py:250
  9.0 1.0 %copy-done = bf16[128,2048]{1,0:T(8,128)(2,1)S(1)} copy-done((bf16[128,2048]{1,0:T(8,128)(2,1)S(1)}, bf16[128,2048]{1,0:T(8,128)(2,1)}, u32[]{:S(2)}) %copy-start) | copy-done | bytes 524312
  10.1 1.0 %copy-done.1 = bf16[128,2048]{1,0:T(8,128)(2,1)S(1)} copy-done((bf16[128,2048]{1,0:T(8,128)(2,1)S(1)}, bf16[128,2048]{1,0:T(8,128)(2,1)}, u32[]{:S(2)}) %copy-start.1) | copy-done | bytes 524312
  11.1 0.3 shard_map.102
  11.4 3.4 %collective-permute-start.5 = (bf16[2048,128]{1,0:T(8,128)(2,1)S(1)}, bf16[2048,128]{1,0:T(8,128)(2,1)S(1)}, u32[]{:S(2)}, u32[]{:S(2)}) collective-permute-start(bf16[2048,128]{1,0:T(8,128)(2,1)S(1)} %get-tuple-element.32), channel_id=1, source_target_pairs={{0,1},{1,0},{2,3},{3,2},{4,5},{5,4},{6,7},{7,6},{8,9},{9,8},{10,11... | collective-permute-start | bytes 1572872 | tf_op jit(solution)/shard_map/ppermute | solution.py:253
  14.8 0.0 collective-permute-done.2.refs_2_.refs_3_
  14.8 1.6 %collective-permute-done.refs_0_.refs_1_ = bf16[136,512]{1,0:T(8,128)(2,1)S(1)} collective-permute-done((bf16[136,512]{1,0:T(8,128)(2,1)S(1)}, bf16[136,512]{1,0:T(8,128)(2,1)S(1)}, u32[]{:S(2)}, u32[]{:S(2)}) %collective-permute-start) | collective-permute-done | bytes 139296 | tf_op jit(solution)/shard_map/ppermute | solution.py:250
  16.4 3.7 %collective-permute-done.1.refs_1_.refs_2_ = bf16[136,512]{1,0:T(8,128)(2,1)S(1)} collective-permute-done((bf16[136,512]{1,0:T(8,128)(2,1)S(1)}, bf16[136,512]{1,0:T(8,128)(2,1)S(1)}, u32[]{:S(2)}, u32[]{:S(2)}) %collective-permute-start.1) | collective-permute-done | bytes 139296 | tf_op jit(solution)/shard_map/ppermute | solution.py:250
  20.1 1.9 %collective-permute-start.4 = (bf16[3,136,512]{2,1,0:T(8,128)(2,1)S(1)}, bf16[3,136,512]{2,1,0:T(8,128)(2,1)S(1)}, u32[]{:S(2)}, u32[]{:S(2)}) collective-permute-start(bf16[3,136,512]{2,1,0:T(8,128)(2,1)S(1)} %shard_map.104), channel_id=1, source_target_pairs={{0,4},{4,8},{8,12},{12,16},{16,20},{20,24},{24,28},{1,5},{5,9},{9,... | collective-permute-start | bytes 1253384 | tf_op jit(solution)/shard_map/ppermute | solution.py:257
  22.1 3.5 %collective-permute-start.3 = (bf16[136,512]{1,0:T(8,128)(2,1)S(1)}, bf16[136,512]{1,0:T(8,128)(2,1)S(1)}, u32[]{:S(2)}, u32[]{:S(2)}) collective-permute-start(bf16[136,512]{1,0:T(8,128)(2,1)S(1)} %get-tuple-element.29.refs_0_), channel_id=1, source_target_pairs={{0,4},{4,8},{8,12},{12,16},{16,20},{20,24},{24,28},{1,5},{5,9},{9,... | collective-permute-start | bytes 417800 | tf_op jit(solution)/shard_map/ppermute | solution.py:254
  25.6 6.3 %collective-permute-done.3.refs_4_ = bf16[136,512]{1,0:T(8,128)(2,1)S(1)} collective-permute-done((bf16[136,512]{1,0:T(8,128)(2,1)S(1)}, bf16[136,512]{1,0:T(8,128)(2,1)S(1)}, u32[]{:S(2)}, u32[]{:S(2)}) %collective-permute-start.3) | collective-permute-done | bytes 139296 | tf_op jit(solution)/shard_map/ppermute | solution.py:254
  31.9 0.0 collective-permute-done.4.refs_5_
  31.9 2.7 %shard_map.105 = (bf16[256,1024]{1,0:T(8,128)(2,1)S(1)}, f32[512,128]{1,0:T(8,128)S(1)}, f32[512,128]{1,0:T(8,128)S(1)}, f32[512,128]{1,0:T(8,128)S(1)}, f32[512...) custom-call(bf16[2048,128]{1,0:T(8,128)(2,1)S(1)} %get-tuple-element.28.qg_ref, ...), custom_call_target="tpu_custom_call" | custom-call | flops 805306368 | bytes 4259840 | tf_op jit(solution)/shard_map/pallas_call | solution.py:25
  34.6 2.8 %shard_map.106 = (bf16[256,1024]{1,0:T(8,128)(2,1)S(1)}, f32[512,128]{1,0:T(8,128)S(1)}, f32[512,128]{1,0:T(8,128)S(1)}, f32[512,128]{1,0:T(8,128)S(1)}, f32[512...) custom-call(bf16[2048,128]{1,0:T(8,128)(2,1)S(1)} %collective-permute-done.5.qg_ref, ...), custom_call_target="tpu_custom_call" | custom-call | flops 805306368 | bytes 5832704 | tf_op jit(solution)/shard_map/pallas_call | solution.py:25
  37.4 1.9 %collective-permute-start.7 = (bf16[4,512,128]{2,1,0:T(8,128)(2,1)S(1)}, bf16[4,512,128]{2,1,0:T(8,128)(2,1)S(1)}, u32[]{:S(2)}, u32[]{:S(2)}) collective-permute-start(bf16[4,512,128]{2,1,0:T(8,128)(2,1)S(1)} %get-tuple-element.41), channel_id=1, source_target_pairs={{4,0},{8,4},{12,8},{16,12},{20,16},{24,20},{28,24},{5,1},{9,5},{13... | collective-permute-start | bytes 1572872 | tf_op jit(solution)/shard_map/ppermute | solution.py:286
  39.3 0.1 collective-permute-start.6
  39.4 6.6 %collective-permute-done.7.far = bf16[4,512,128]{2,1,0:T(8,128)(2,1)S(1)} collective-permute-done((bf16[4,512,128]{2,1,0:T(8,128)(2,1)S(1)}, bf16[4,512,128]{2,1,0:T(8,128)(2,1)S(1)}, u32[]{:S(2)}, u32[]{:S(2)}) %collective-permute-start.7) | collective-permute-done | bytes 524320 | tf_op jit(solution)/shard_map/ppermute | solution.py:286
  46.0 0.1 shard_map.108
  46.1 2.5 %collective-permute-start.8 = (bf16[512,128]{1,0:T(8,128)(2,1)S(1)}, bf16[512,128]{1,0:T(8,128)(2,1)S(1)}, u32[]{:S(2)}, u32[]{:S(2)}) collective-permute-start(bf16[512,128]{1,0:T(8,128)(2,1)S(1)} %get-tuple-element.47), channel_id=1, source_target_pairs={{0,3},{1,0},{2,1},{3,2},{4,7},{5,4},{6,5},{7,6},{8,11},{9,8},{10,9... | collective-permute-start | bytes 393224 | tf_op jit(solution)/shard_map/ppermute | solution.py:293
  48.5 0.9 %collective-permute-start.10 = (bf16[512,128]{1,0:T(8,128)(2,1)S(1)}, bf16[512,128]{1,0:T(8,128)(2,1)S(1)}, u32[]{:S(2)}, u32[]{:S(2)}) collective-permute-start(bf16[512,128]{1,0:T(8,128)(2,1)S(1)} %get-tuple-element.49), channel_id=1, source_target_pairs={{0,1},{1,2},{2,3},{3,0},{4,5},{5,6},{6,7},{7,4},{8,9},{9,10},{10,1... | collective-permute-start | bytes 393224 | tf_op jit(solution)/shard_map/ppermute | solution.py:293
  49.4 7.5 %collective-permute-done.6.other_ref = bf16[256,1024]{1,0:T(8,128)(2,1)S(1)} collective-permute-done((bf16[256,1024]{1,0:T(8,128)(2,1)S(1)}, bf16[256,1024]{1,0:T(8,128)(2,1)S(1)}, u32[]{:S(2)}, u32[]{:S(2)}) %collective-permute-start.6) | collective-permute-done | bytes 524320 | tf_op jit(solution)/shard_map/ppermute | solution.py:287
  57.0 1.0 %shard_map.107 = (bf16[128,2048]{1,0:T(8,128)(2,1)}, bf16[128,2048]{1,0:T(8,128)(2,1)}) custom-call(bf16[256,1024]{1,0:T(8,128)(2,1)S(1)} %get-tuple-element.31.mine_ref, bf16[256,1024]{1,0:T(8,128)(2,1)S(1)} %collective-permute-done.6.other_ref), custom_call_target="tpu_custom_call" | custom-call | bytes 2097152 | tf_op jit(solution)/shard_map/pallas_call | solution.py:25
  58.0 1.3 %collective-permute-done.8.refs_1_ = bf16[512,128]{1,0:T(8,128)(2,1)S(1)} collective-permute-done((bf16[512,128]{1,0:T(8,128)(2,1)S(1)}, bf16[512,128]{1,0:T(8,128)(2,1)S(1)}, u32[]{:S(2)}, u32[]{:S(2)}) %collective-permute-start.8) | collective-permute-done | bytes 131104 | tf_op jit(solution)/shard_map/ppermute | solution.py:293
  59.3 3.5 %collective-permute-done.10.refs_3_ = bf16[512,128]{1,0:T(8,128)(2,1)S(1)} collective-permute-done((bf16[512,128]{1,0:T(8,128)(2,1)S(1)}, bf16[512,128]{1,0:T(8,128)(2,1)S(1)}, u32[]{:S(2)}, u32[]{:S(2)}) %collective-permute-start.10) | collective-permute-done | bytes 131104 | tf_op jit(solution)/shard_map/ppermute | solution.py:293
  62.9 0.8 %shard_map.109 = (bf16[128,512]{1,0:T(8,128)(2,1)}, bf16[128,512]{1,0:T(8,128)(2,1)}) custom-call(f32[512,128]{1,0:T(8,128)S(1)} %get-tuple-element.46.refs_0_, bf16[512,128]{1,0:T(8,128)(2,1)S(1)} %collective-permute-done.8.refs_1_, bf16[512,128]{1,0:T(8,128)(2,1)S(1)} %collective-permute-done.9.refs_2_, bf16[512,128]{1,0:T(8,128)(2,1)S(1)} %collective-permute-done.10.refs_3_), custom_call_target="tpu_custom_call" | custom-call | bytes 917504 | tf_op jit(solution)/shard_map/pallas_call | solution.py:25
  (10 shorter events, 0.0 us)
Async XLA Ops:
  1.3 0.7 %copy-start.4 = (s32[1,4]{1,0:T(1,128)S(1)}, s32[1,4]{1,0:T(1,128)}, u32[]{:S(2)}) copy-start(s32[1,4]{1,0:T(1,128)} %ids_ref.1) | copy-start | bytes 52
  1.3 0.7 %copy-start.5 = (s32[128]{0:T(128)S(1)}, s32[128]{0:T(128)}, u32[]{:S(2)}) copy-start(s32[128]{0:T(128)} %param.11) | copy-start | bytes 1540
  2.0 0.9 %copy-start.2 = (bf16[128,512]{1,0:T(8,128)(2,1)S(1)}, bf16[128,512]{1,0:T(8,128)(2,1)}, u32[]{:S(2)}) copy-start(bf16[128,512]{1,0:T(8,128)(2,1)} %k_ref.1) | copy-start | bytes 393220
  2.9 0.9 %copy-start.3 = (bf16[128,512]{1,0:T(8,128)(2,1)S(1)}, bf16[128,512]{1,0:T(8,128)(2,1)}, u32[]{:S(2)}) copy-start(bf16[128,512]{1,0:T(8,128)(2,1)} %v_ref.1) | copy-start | bytes 393220
  4.3 10.5 %collective-permute-start.2 = (bf16[136,512]{1,0:T(8,128)(2,1)S(1)}, bf16[136,512]{1,0:T(8,128)(2,1)S(1)}, u32[]{:S(2)}, u32[]{:S(2)}) collective-permute-start(bf16[136,512]{1,0:T(8,128)(2,1)S(1)} %get-tuple-element.30), channel_id=1, source_target_pairs={{0,3},{1,0},{2,1},{3,2},{4,7},{5,4},{6,5},{7,6},{8,11},{9,8},{10,9... | collective-permute-start | bytes 417800 | tf_op jit(solution)/shard_map/ppermute | solution.py:250
  8.0 8.4 %collective-permute-start = (bf16[136,512]{1,0:T(8,128)(2,1)S(1)}, bf16[136,512]{1,0:T(8,128)(2,1)S(1)}, u32[]{:S(2)}, u32[]{:S(2)}) collective-permute-start(bf16[136,512]{1,0:T(8,128)(2,1)S(1)} %get-tuple-element.30), channel_id=1, source_target_pairs={{0,1},{1,2},{2,3},{3,0},{4,5},{5,6},{6,7},{7,4},{8,9},{9,10},{10,1... | collective-permute-start | bytes 417800 | tf_op jit(solution)/shard_map/ppermute | solution.py:250
  8.0 12.1 %collective-permute-start.1 = (bf16[136,512]{1,0:T(8,128)(2,1)S(1)}, bf16[136,512]{1,0:T(8,128)(2,1)S(1)}, u32[]{:S(2)}, u32[]{:S(2)}) collective-permute-start(bf16[136,512]{1,0:T(8,128)(2,1)S(1)} %get-tuple-element.29.refs_0_), channel_id=1, source_target_pairs={{0,2},{1,3},{2,0},{3,1},{4,6},{5,7},{6,4},{7,5},{8,10},{9,11},{10,... | collective-permute-start | bytes 417800 | tf_op jit(solution)/shard_map/ppermute | solution.py:250
  9.0 1.0 %copy-start = (bf16[128,2048]{1,0:T(8,128)(2,1)S(1)}, bf16[128,2048]{1,0:T(8,128)(2,1)}, u32[]{:S(2)}) copy-start(bf16[128,2048]{1,0:T(8,128)(2,1)} %q_ref.1) | copy-start | bytes 1572868
  10.0 1.0 %copy-start.1 = (bf16[128,2048]{1,0:T(8,128)(2,1)S(1)}, bf16[128,2048]{1,0:T(8,128)(2,1)}, u32[]{:S(2)}) copy-start(bf16[128,2048]{1,0:T(8,128)(2,1)} %g_ref.1) | copy-start | bytes 1572868
  11.4 23.2 %collective-permute-start.5 = (bf16[2048,128]{1,0:T(8,128)(2,1)S(1)}, bf16[2048,128]{1,0:T(8,128)(2,1)S(1)}, u32[]{:S(2)}, u32[]{:S(2)}) collective-permute-start(bf16[2048,128]{1,0:T(8,128)(2,1)S(1)} %get-tuple-element.32), channel_id=1, source_target_pairs={{0,1},{1,0},{2,3},{3,2},{4,5},{5,4},{6,7},{7,6},{8,9},{9,8},{10,11... | collective-permute-start | bytes 1572872 | tf_op jit(solution)/shard_map/ppermute | solution.py:253
  20.1 11.8 %collective-permute-start.4 = (bf16[3,136,512]{2,1,0:T(8,128)(2,1)S(1)}, bf16[3,136,512]{2,1,0:T(8,128)(2,1)S(1)}, u32[]{:S(2)}, u32[]{:S(2)}) collective-permute-start(bf16[3,136,512]{2,1,0:T(8,128)(2,1)S(1)} %shard_map.104), channel_id=1, source_target_pairs={{0,4},{4,8},{8,12},{12,16},{16,20},{20,24},{24,28},{1,5},{5,9},{9,... | collective-permute-start | bytes 1253384 | tf_op jit(solution)/shard_map/ppermute | solution.py:257
  22.1 9.8 %collective-permute-start.3 = (bf16[136,512]{1,0:T(8,128)(2,1)S(1)}, bf16[136,512]{1,0:T(8,128)(2,1)S(1)}, u32[]{:S(2)}, u32[]{:S(2)}) collective-permute-start(bf16[136,512]{1,0:T(8,128)(2,1)S(1)} %get-tuple-element.29.refs_0_), channel_id=1, source_target_pairs={{0,4},{4,8},{8,12},{12,16},{16,20},{20,24},{24,28},{1,5},{5,9},{9,... | collective-permute-start | bytes 417800 | tf_op jit(solution)/shard_map/ppermute | solution.py:254
  37.4 8.6 %collective-permute-start.7 = (bf16[4,512,128]{2,1,0:T(8,128)(2,1)S(1)}, bf16[4,512,128]{2,1,0:T(8,128)(2,1)S(1)}, u32[]{:S(2)}, u32[]{:S(2)}) collective-permute-start(bf16[4,512,128]{2,1,0:T(8,128)(2,1)S(1)} %get-tuple-element.41), channel_id=1, source_target_pairs={{4,0},{8,4},{12,8},{16,12},{20,16},{24,20},{28,24},{5,1},{9,5},{13... | collective-permute-start | bytes 1572872 | tf_op jit(solution)/shard_map/ppermute | solution.py:286
  39.3 17.7 %collective-permute-start.6 = (bf16[256,1024]{1,0:T(8,128)(2,1)S(1)}, bf16[256,1024]{1,0:T(8,128)(2,1)S(1)}, u32[]{:S(2)}, u32[]{:S(2)}) collective-permute-start(bf16[256,1024]{1,0:T(8,128)(2,1)S(1)} %get-tuple-element.38), channel_id=1, source_target_pairs={{0,1},{1,0},{2,3},{3,2},{4,5},{5,4},{6,7},{7,6},{8,9},{9,8},{10,11... | collective-permute-start | bytes 1572872 | tf_op jit(solution)/shard_map/ppermute | solution.py:287
  46.1 13.2 %collective-permute-start.8 = (bf16[512,128]{1,0:T(8,128)(2,1)S(1)}, bf16[512,128]{1,0:T(8,128)(2,1)S(1)}, u32[]{:S(2)}, u32[]{:S(2)}) collective-permute-start(bf16[512,128]{1,0:T(8,128)(2,1)S(1)} %get-tuple-element.47), channel_id=1, source_target_pairs={{0,3},{1,0},{2,1},{3,2},{4,7},{5,4},{6,5},{7,6},{8,11},{9,8},{10,9... | collective-permute-start | bytes 393224 | tf_op jit(solution)/shard_map/ppermute | solution.py:293
  48.5 10.8 %collective-permute-start.9 = (bf16[512,128]{1,0:T(8,128)(2,1)S(1)}, bf16[512,128]{1,0:T(8,128)(2,1)S(1)}, u32[]{:S(2)}, u32[]{:S(2)}) collective-permute-start(bf16[512,128]{1,0:T(8,128)(2,1)S(1)} %get-tuple-element.48), channel_id=1, source_target_pairs={{0,2},{1,3},{2,0},{3,1},{4,6},{5,7},{6,4},{7,5},{8,10},{9,11},{10,... | collective-permute-start | bytes 393224 | tf_op jit(solution)/shard_map/ppermute | solution.py:293
  48.5 14.3 %collective-permute-start.10 = (bf16[512,128]{1,0:T(8,128)(2,1)S(1)}, bf16[512,128]{1,0:T(8,128)(2,1)S(1)}, u32[]{:S(2)}, u32[]{:S(2)}) collective-permute-start(bf16[512,128]{1,0:T(8,128)(2,1)S(1)} %get-tuple-element.49), channel_id=1, source_target_pairs={{0,1},{1,2},{2,3},{3,0},{4,5},{5,6},{6,7},{7,4},{8,9},{9,10},{10,1... | collective-permute-start | bytes 393224 | tf_op jit(solution)/shard_map/ppermute | solution.py:293

commit v3 on v2

--- a/solution.py
+++ b/solution.py
@@ -13,6 +13,7 @@
 BLOCK_ROWS = 64
 NEG = -1e30
 LOG2E = 1.4426950408889634
+
 
 VMEM = pl.BlockSpec(memory_space=pltpu.VMEM)
 SMEM = pl.BlockSpec(memory_space=pltpu.SMEM)
@@ -79,13 +80,26 @@
         refs[-1][i] = ref[...]
 
 
-def attend_kernel(heads, group, partner, qg_ref, *refs):
-    pool, far0, farm = refs[:group], refs[group], refs[group + 1]
-    refs = refs[group + 2 :]
+def merge(arrays):
+    out = jax.ShapeDtypeStruct((len(arrays), *arrays[0].shape), arrays[0].dtype)
+    return call(merge_kernel, [out], arrays)[0]
+
+
+def entries(refs, groups):
+    places = {d: ref.at[i] for ref, group in zip(refs, groups) for i, d in enumerate(group)}
+    return [places[d] for d in sorted(places)]
+
+
+def attend_kernel(heads, group, far_in, far_out, partner, qg_ref, *refs):
+    pool, refs = refs[:group], refs[group:]
+    far_pool, refs = entries(refs[: len(far_in)], far_in), refs[len(far_in) :]
+    parts = group + len(far_out)
     if partner:
-        before, refs = refs[: group + 1], refs[group + 1 :]
-    ag_ref, near, far = refs[0], refs[1 : 1 + group], refs[1 + group]
-    kv_s, seg_s, bias_s, term_s, p_s, dp_s, w_s, ds_s = refs[2 + group :]
+        old, refs = refs[:parts], refs[parts:]
+        old = [*old[:group], *entries(old[group:], far_out)]
+    ag_ref, out, refs = refs[0], refs[1 : 1 + parts], refs[1 + parts :]
+    out = [*out[:group], *entries(out[group:], far_out)]
+    kv_s, seg_s, bias_s, term_s, p_s, dp_s, w_s, ds_s = refs
     slots, width, tile = term_s.shape
     half = width // 2
     size = half // heads
@@ -117,8 +131,7 @@
             kv_s[j * tile : (j + 1) * tile, :] = jnp.zeros((tile, width), BF16)
             seg_s[j] = jnp.full(seg_s.shape[1:], -1.0, F32)
 
-    far_pool = [far0] + [farm.at[d] for d in range(group - 1)]
-    for slot, source in zip(near_slot + far_slot, list(pool) + far_pool):
+    for slot, source in zip(near_slot + far_slot, [*pool, *far_pool]):
 
         @pl.when(slot >= 0)
         def _():
@@ -176,20 +189,17 @@
         weigh(h)
         finish(h)
 
-    far_out = [far.at[d] for d in range(group)]
-    if partner:
-        old = list(before[:group]) + [before[group].at[d] for d in range(group)]
-    for i, (slot, out) in enumerate(zip(near_slot + far_slot, list(near) + far_out)):
+    for i, slot in enumerate(near_slot + far_slot):
 
         @pl.when(slot >= 0)
         def _():
             new = term_s[slot].astype(F32)
-            out[...] = (new + old[i][...] if partner else new).astype(out.dtype)
+            out[i][...] = (new + old[i][...] if partner else new).astype(out[i].dtype)
 
         @pl.when(slot < 0)
         def _():
             new = old[i][...] if partner else jnp.zeros((width, tile), F32)
-            out[...] = new.astype(out.dtype)
+            out[i][...] = new.astype(out[i].dtype)
 
 
 def join_kernel(far, *refs):
@@ -220,6 +230,11 @@
     for index, ref in ((parity(), mine_ref), (1 - parity(), other_ref)):
         att_ref[:, part_of(index, half)] = ref[0:tile, :]
         gq_ref[:, part_of(index, half)] = ref[tile:, :]
+
+
+def turns_of(group):
+    turns = sorted(range(1, group), key=lambda d: (min(d, group - d), d))
+    return turns[:2], turns[2:]
 
 
 def body(queries, keys, values, grad_out, segments, block_ids, block_count):
@@ -238,23 +253,27 @@
     ring = lambda d: [(i, (i + d) % group) for i in range(group)]
     partners = [(i, i + 1 - 2 * (i % PAIR)) for i in range(group)]
 
+    queries, keys, values, grad_out, segments, block_ids = (
+        pltpu.with_memory_space_constraint(x, pltpu.HBM)
+        for x in (queries, keys, values, grad_out, segments.reshape(1, tile), block_ids)
+    )
     payload = shape((tile + -(-(slots + 2) // 8) * 8, width), BF16)
     mine, other = call(
         functools.partial(pack_kernel, group),
         [payload] * 2,
-        [block_ids, block_count, keys, values, segments.reshape(1, tile)],
+        [block_ids, block_count, keys, values, segments],
         in_specs=[SMEM] * 2 + [VMEM] * 3,
     )
+    first, rest = turns_of(group)
     near = [mine]
     for d in range(1, group):
         near.append(lax.ppermute(other if d % PAIR else mine, "grp", ring(d)))
     qg = shape((2 * heads * rows, size), BF16)
     qg_mine, qg_other = call(split_kernel, [qg] * 2, [queries, grad_out])
     qg_partner = lax.ppermute(qg_other, "grp", partners)
-    far0 = lax.ppermute(mine, "cp", ahead)
-    merged = shape((group - 1, *payload.shape), BF16)
-    (merged,) = call(merge_kernel, [merged], near[1:])
-    farm = lax.ppermute(merged, "cp", ahead)
+    far_in = [g for g in ([0], first, rest) if g]
+    far = [lax.ppermute(merge([near[d] for d in g]), "cp", ahead) for g in far_in]
+    far_out = [g for g in (first, [0] + rest) if g]
 
     ag = shape((2 * tile, full // PAIR), BF16)
     term = shape((width, tile), F32)
@@ -269,25 +288,24 @@
         pltpu.VMEM((heads, rows, slots * tile), BF16),
     ]
     flops = 12 * heads * rows * slots * tile * size
-    ag_mine, *terms = call(
-        functools.partial(attend_kernel, heads, group, False),
-        [ag] + [term] * group + [shape((group, width, tile), F32)],
-        [qg_mine, *near, far0, farm],
-        scratch=scratch,
-        flops=flops,
-    )
-    ag_partner, *terms = call(
-        functools.partial(attend_kernel, heads, group, True),
-        [ag] + [term] * group + [shape((group, width, tile), BF16)],
-        [qg_partner, *near, far0, farm, *terms],
-        scratch=scratch,
-        flops=flops,
-    )
-    later = lax.ppermute(terms[group], "cp", back)
+
+    def attend(qg, before, dtype):
+        return call(
+            functools.partial(attend_kernel, heads, group, far_in, far_out, bool(before)),
+            [ag] + [term] * group + [shape((len(g), width, tile), dtype) for g in far_out],
+            [qg, *near, *far, *before],
+            scratch=scratch,
+            flops=flops,
+        )
+
+    ag_mine, *terms = attend(qg_mine, [], F32)
+    ag_partner, *terms = attend(qg_partner, terms, BF16)
     ag_back = lax.ppermute(ag_partner, "grp", partners)
-    joined = call(
-        join_kernel, [term] + [shape((width, tile), BF16)] * (group - 1), [later, *terms[:group]]
-    )
+    joined = {}
+    for g, far_terms in zip(far_out, terms[group:]):
+        later = lax.ppermute(far_terms, "cp", back)
+        outs = [term if d == 0 else shape((width, tile), BF16) for d in g]
+        joined.update(zip(g, call(join_kernel, outs, [later] + [terms[d] for d in g])))
     sums = [joined[0]]
     for d in range(1, group):
         sums.append(lax.ppermute(joined[d], "grp", ring(-d)))

time: 64 us -> 67.8 us (1.059)
  the two profiles are of different devices: /device:TPU:4 before, /device:TPU:3 now
where the time goes in v3:
time: 67.8 us; the launch traced here: 67.5 us
  waiting for transfers between devices  28.4 us (42%)
  starting transfers between devices  27.8 us (41%)
  Pallas kernels  9.9 us (15%)
  between operations  1.42 us (2%)
    ppermute x3, waiting for transfers between devices, body(): near.append(lax.ppermute(other if d % PAIR else mine, 'grp', ring(d)))  14 us
    ppermute x3, starting transfers between devices, body(): lax.ppermute(merge([near[d] for d in g]), 'cp', ahead)  11.1 us
    pallas_call x11, Pallas kernels, call(): pl.pallas_call(kernel, out_shape=outs, in_specs=in_specs or [VMEM] * len(...  9.9 us
    ppermute x3, waiting for transfers between devices, body(): sums.append(lax.ppermute(joined[d], 'grp', ring(-d)))  8.27 us
    ppermute x3, starting transfers between devices, body(): sums.append(lax.ppermute(joined[d], 'grp', ring(-d)))  6.26 us
    ppermute x2, starting transfers between devices, body(): later = lax.ppermute(far_terms, 'cp', back)  5.2 us
    ppermute x2, waiting for transfers between devices, body(): later = lax.ppermute(far_terms, 'cp', back)  4.12 us
    ppermute x3, starting transfers between devices, body(): near.append(lax.ppermute(other if d % PAIR else mine, 'grp', ring(d)))  3.83 us
  transfers between devices with their start and end apart: 13, of which 7 were waited for; matrix products, arithmetic and copies ran while one was open for 0% of the time, Pallas kernels for 7%

profile of v3, /device:TPU:3, one launch (start us, length us, event | category | flops | bytes accessed | tf_op | source)
XLA Modules:
  0.0 67.5 jit_solution(11881321268368312910)
XLA Ops:
  0.6 1.5 %shard_map.102 = (bf16[2048,128]{1,0:T(8,128)(2,1)S(1)}, bf16[2048,128]{1,0:T(8,128)(2,1)S(1)}) custom-call(bf16[128,2048]{1,0:T(8,128)(2,1)} %q_ref.1, bf16[128,2048]{1,0:T(8,128)(2,1)} %g_ref.1), custom_call_target="tpu_custom_call" | custom-call | bytes 2097152 | tf_op jit(solution)/shard_map/pallas_call | solution.py:26
  2.1 1.4 %collective-permute-start.6 = (bf16[2048,128]{1,0:T(8,128)(2,1)S(1)}, bf16[2048,128]{1,0:T(8,128)(2,1)S(1)}, u32[]{:S(2)}, u32[]{:S(2)}) collective-permute-start(bf16[2048,128]{1,0:T(8,128)(2,1)S(1)} %get-tuple-element.34), channel_id=1, source_target_pairs={{0,1},{1,0},{2,3},{3,2},{4,5},{5,4},{6,7},{7,6},{8,9},{9,8},{10,11... | collective-permute-start | bytes 1572872 | tf_op jit(solution)/shard_map/ppermute | solution.py:273
  4.1 1.0 %shard_map.103 = (bf16[136,512]{1,0:T(8,128)(2,1)S(1)}, bf16[136,512]{1,0:T(8,128)(2,1)S(1)}) custom-call(s32[1,4]{1,0:T(1,128)} %ids_ref.1, s32[1]{0:T(128)S(6)} %copy.11.count_ref, bf16[128,512]{1,0:T(8,128)(2,1)} %k_ref.1, bf16[128,512]{1,0:T(8,128)(2,1)} %v_ref.1, s32[1,128]{1,0:T(1,128)} %bitcast.1), custom_call_target="tpu_custom_call" | custom-call | bytes 541204 | tf_op jit(solution)/shard_map/pallas_call | solution.py:26
  5.1 2.2 %collective-permute-start.2 = (bf16[136,512]{1,0:T(8,128)(2,1)S(1)}, bf16[136,512]{1,0:T(8,128)(2,1)S(1)}, u32[]{:S(2)}, u32[]{:S(2)}) collective-permute-start(bf16[136,512]{1,0:T(8,128)(2,1)S(1)} %get-tuple-element.32), channel_id=1, source_target_pairs={{0,3},{1,0},{2,1},{3,2},{4,7},{5,4},{6,5},{7,6},{8,11},{9,8},{10,9... | collective-permute-start | bytes 417800 | tf_op jit(solution)/shard_map/ppermute | solution.py:270
  7.4 0.0 collective-permute-start
  7.4 1.6 %collective-permute-start.1 = (bf16[136,512]{1,0:T(8,128)(2,1)S(1)}, bf16[136,512]{1,0:T(8,128)(2,1)S(1)}, u32[]{:S(2)}, u32[]{:S(2)}) collective-permute-start(bf16[136,512]{1,0:T(8,128)(2,1)S(1)} %get-tuple-element.31.refs_0_), channel_id=1, source_target_pairs={{0,2},{1,3},{2,0},{3,1},{4,6},{5,7},{6,4},{7,5},{8,10},{9,11},{10,... | collective-permute-start | bytes 417800 | tf_op jit(solution)/shard_map/ppermute | solution.py:270
  9.0 12.9 %collective-permute-done.2.refs_1_.refs_3_ = bf16[136,512]{1,0:T(8,128)(2,1)S(1)} collective-permute-done((bf16[136,512]{1,0:T(8,128)(2,1)S(1)}, bf16[136,512]{1,0:T(8,128)(2,1)S(1)}, u32[]{:S(2)}, u32[]{:S(2)}) %collective-permute-start.2) | collective-permute-done | bytes 139296 | tf_op jit(solution)/shard_map/ppermute | solution.py:270
  21.9 1.1 %collective-permute-done.refs_0_.refs_1_ = bf16[136,512]{1,0:T(8,128)(2,1)S(1)} collective-permute-done((bf16[136,512]{1,0:T(8,128)(2,1)S(1)}, bf16[136,512]{1,0:T(8,128)(2,1)S(1)}, u32[]{:S(2)}, u32[]{:S(2)}) %collective-permute-start) | collective-permute-done | bytes 139296 | tf_op jit(solution)/shard_map/ppermute | solution.py:270
  23.0 5.7 %collective-permute-start.4 = (bf16[2,136,512]{2,1,0:T(8,128)(2,1)S(1)}, bf16[2,136,512]{2,1,0:T(8,128)(2,1)S(1)}, u32[]{:S(2)}, u32[]{:S(2)}) collective-permute-start(bf16[2,136,512]{2,1,0:T(8,128)(2,1)S(1)} %shard_map.105), channel_id=1, source_target_pairs={{0,4},{4,8},{8,12},{12,16},{16,20},{20,24},{24,28},{1,5},{5,9},{9,... | collective-permute-start | bytes 835592 | tf_op jit(solution)/shard_map/ppermute | solution.py:275
  28.7 1.9 %collective-permute-start.3 = (bf16[1,136,512]{2,1,0:T(8,128)(2,1)S(1)}, bf16[1,136,512]{2,1,0:T(8,128)(2,1)S(1)}, u32[]{:S(2)}, u32[]{:S(2)}) collective-permute-start(bf16[1,136,512]{2,1,0:T(8,128)(2,1)S(1)} %shard_map.104), channel_id=1, source_target_pairs={{0,4},{4,8},{8,12},{12,16},{16,20},{20,24},{24,28},{1,5},{5,9},{9,... | collective-permute-start | bytes 417800 | tf_op jit(solution)/shard_map/ppermute | solution.py:275
  30.6 0.0 collective-permute-done.1.refs_0_.refs_2_
  30.6 3.5 %collective-permute-start.5 = (bf16[1,136,512]{2,1,0:T(8,128)(2,1)S(1)}, bf16[1,136,512]{2,1,0:T(8,128)(2,1)S(1)}, u32[]{:S(2)}, u32[]{:S(2)}) collective-permute-start(bf16[1,136,512]{2,1,0:T(8,128)(2,1)S(1)} %shard_map.106), channel_id=1, source_target_pairs={{0,4},{4,8},{8,12},{12,16},{16,20},{20,24},{24,28},{1,5},{5,9},{9,... | collective-permute-start | bytes 417800 | tf_op jit(solution)/shard_map/ppermute | solution.py:275
  34.2 0.0 collective-permute-done.3.refs_4_
  34.2 2.0 %collective-permute-done.5.refs_6_ = bf16[1,136,512]{2,1,0:T(8,128)(2,1)S(1)} collective-permute-done((bf16[1,136,512]{2,1,0:T(8,128)(2,1)S(1)}, bf16[1,136,512]{2,1,0:T(8,128)(2,1)S(1)}, u32[]{:S(2)}, u32[]{:S(2)}) %collective-permute-start.5) | collective-permute-done | bytes 139296 | tf_op jit(solution)/shard_map/ppermute | solution.py:275
  36.2 0.0 collective-permute-done.4.refs_5_
  36.2 2.7 %shard_map.107 = (bf16[256,1024]{1,0:T(8,128)(2,1)S(1)}, f32[512,128]{1,0:T(8,128)S(1)}, f32[512,128]{1,0:T(8,128)S(1)}, f32[512,128]{1,0:T(8,128)S(1)}, f32[512...) custom-call(bf16[2048,128]{1,0:T(8,128)(2,1)S(1)} %get-tuple-element.30.qg_ref, ...), custom_call_target="tpu_custom_call" | custom-call | flops 805306368 | bytes 4259840 | tf_op jit(solution)/shard_map/pallas_call | solution.py:26
  38.9 0.0 collective-permute-done.6.qg_ref
  38.9 2.7 %shard_map.108 = (bf16[256,1024]{1,0:T(8,128)(2,1)S(1)}, f32[512,128]{1,0:T(8,128)S(1)}, f32[512,128]{1,0:T(8,128)S(1)}, f32[512,128]{1,0:T(8,128)S(1)}, f32[512...) custom-call(bf16[2048,128]{1,0:T(8,128)(2,1)S(1)} %collective-permute-done.6.qg_ref, ...), custom_call_target="tpu_custom_call" | custom-call | flops 805306368 | bytes 5832704 | tf_op jit(solution)/shard_map/pallas_call | solution.py:26
  41.6 0.1 collective-permute-start.7
  41.7 3.3 %collective-permute-start.8 = (bf16[2,512,128]{2,1,0:T(8,128)(2,1)S(1)}, bf16[2,512,128]{2,1,0:T(8,128)(2,1)S(1)}, u32[]{:S(2)}, u32[]{:S(2)}) collective-permute-start(bf16[2,512,128]{2,1,0:T(8,128)(2,1)S(1)} %get-tuple-element.44), channel_id=1, source_target_pairs={{4,0},{8,4},{12,8},{16,12},{20,16},{24,20},{28,24},{5,1},{9,5},{13... | collective-permute-start | bytes 786440 | tf_op jit(solution)/shard_map/ppermute | solution.py:306
  45.0 1.9 %collective-permute-start.9 = (bf16[2,512,128]{2,1,0:T(8,128)(2,1)S(1)}, bf16[2,512,128]{2,1,0:T(8,128)(2,1)S(1)}, u32[]{:S(2)}, u32[]{:S(2)}) collective-permute-start(bf16[2,512,128]{2,1,0:T(8,128)(2,1)S(1)} %get-tuple-element.48), channel_id=1, source_target_pairs={{4,0},{8,4},{12,8},{16,12},{20,16},{24,20},{28,24},{5,1},{9,5},{13... | collective-permute-start | bytes 786440 | tf_op jit(solution)/shard_map/ppermute | solution.py:306
  46.9 4.1 %collective-permute-done.8.far = bf16[2,512,128]{2,1,0:T(8,128)(2,1)S(1)} collective-permute-done((bf16[2,512,128]{2,1,0:T(8,128)(2,1)S(1)}, bf16[2,512,128]{2,1,0:T(8,128)(2,1)S(1)}, u32[]{:S(2)}, u32[]{:S(2)}) %collective-permute-start.8) | collective-permute-done | bytes 262176 | tf_op jit(solution)/shard_map/ppermute | solution.py:306
  51.1 3.8 %collective-permute-start.11 = (bf16[512,128]{1,0:T(8,128)(2,1)S(1)}, bf16[512,128]{1,0:T(8,128)(2,1)S(1)}, u32[]{:S(2)}, u32[]{:S(2)}) collective-permute-start(bf16[512,128]{1,0:T(8,128)(2,1)S(1)} %get-tuple-element.52), channel_id=1, source_target_pairs={{0,2},{1,3},{2,0},{3,1},{4,6},{5,7},{6,4},{7,5},{8,10},{9,11},{10,... | collective-permute-start | bytes 393224 | tf_op jit(solution)/shard_map/ppermute | solution.py:311
  54.8 0.0 collective-permute-done.9.far
  54.9 2.5 %collective-permute-start.10 = (bf16[512,128]{1,0:T(8,128)(2,1)S(1)}, bf16[512,128]{1,0:T(8,128)(2,1)S(1)}, u32[]{:S(2)}, u32[]{:S(2)}) collective-permute-start(bf16[512,128]{1,0:T(8,128)(2,1)S(1)} %get-tuple-element.51), channel_id=1, source_target_pairs={{0,3},{1,0},{2,1},{3,2},{4,7},{5,4},{6,5},{7,6},{8,11},{9,8},{10,9... | collective-permute-start | bytes 393224 | tf_op jit(solution)/shard_map/ppermute | solution.py:311
  57.4 0.0 collective-permute-start.12
  57.4 3.6 %collective-permute-done.11.refs_2_ = bf16[512,128]{1,0:T(8,128)(2,1)S(1)} collective-permute-done((bf16[512,128]{1,0:T(8,128)(2,1)S(1)}, bf16[512,128]{1,0:T(8,128)(2,1)S(1)}, u32[]{:S(2)}, u32[]{:S(2)}) %collective-permute-start.11) | collective-permute-done | bytes 131104 | tf_op jit(solution)/shard_map/ppermute | solution.py:311
  60.9 0.2 collective-permute-done.10.refs_1_
  61.1 4.5 %collective-permute-done.12.refs_3_ = bf16[512,128]{1,0:T(8,128)(2,1)S(1)} collective-permute-done((bf16[512,128]{1,0:T(8,128)(2,1)S(1)}, bf16[512,128]{1,0:T(8,128)(2,1)S(1)}, u32[]{:S(2)}, u32[]{:S(2)}) %collective-permute-start.12) | collective-permute-done | bytes 131104 | tf_op jit(solution)/shard_map/ppermute | solution.py:311
  65.6 0.8 %shard_map.112 = (bf16[128,512]{1,0:T(8,128)(2,1)}, bf16[128,512]{1,0:T(8,128)(2,1)}) custom-call(f32[512,128]{1,0:T(8,128)S(1)} %get-tuple-element.47.refs_0_, bf16[512,128]{1,0:T(8,128)(2,1)S(1)} %collective-permute-done.10.refs_1_, bf16[512,128]{1,0:T(8,128)(2,1)S(1)} %collective-permute-done.11.refs_2_, bf16[512,128]{1,0:T(8,128)(2,1)S(1)} %collective-permute-done.12.refs_3_), custom_call_target="tpu_custom_call" | custom-call | bytes 917504 | tf_op jit(solution)/shard_map/pallas_call | solution.py:26
  66.5 0.0 collective-permute-done.7.other_ref
  66.5 1.0 %shard_map.109 = (bf16[128,2048]{1,0:T(8,128)(2,1)}, bf16[128,2048]{1,0:T(8,128)(2,1)}) custom-call(bf16[256,1024]{1,0:T(8,128)(2,1)S(1)} %get-tuple-element.33.mine_ref, bf16[256,1024]{1,0:T(8,128)(2,1)S(1)} %collective-permute-done.7.other_ref), custom_call_target="tpu_custom_call" | custom-call | bytes 2097152 | tf_op jit(solution)/shard_map/pallas_call | solution.py:26
  (5 shorter events, 0.1 us)
Async XLA Ops:
  2.1 36.8 %collective-permute-start.6 = (bf16[2048,128]{1,0:T(8,128)(2,1)S(1)}, bf16[2048,128]{1,0:T(8,128)(2,1)S(1)}, u32[]{:S(2)}, u32[]{:S(2)}) collective-permute-start(bf16[2048,128]{1,0:T(8,128)(2,1)S(1)} %get-tuple-element.34), channel_id=1, source_target_pairs={{0,1},{1,0},{2,3},{3,2},{4,5},{5,4},{6,7},{7,6},{8,9},{9,8},{10,11... | collective-permute-start | bytes 1572872 | tf_op jit(solution)/shard_map/ppermute | solution.py:273
  5.1 16.8 %collective-permute-start.2 = (bf16[136,512]{1,0:T(8,128)(2,1)S(1)}, bf16[136,512]{1,0:T(8,128)(2,1)S(1)}, u32[]{:S(2)}, u32[]{:S(2)}) collective-permute-start(bf16[136,512]{1,0:T(8,128)(2,1)S(1)} %get-tuple-element.32), channel_id=1, source_target_pairs={{0,3},{1,0},{2,1},{3,2},{4,7},{5,4},{6,5},{7,6},{8,11},{9,8},{10,9... | collective-permute-start | bytes 417800 | tf_op jit(solution)/shard_map/ppermute | solution.py:270
  7.4 15.6 %collective-permute-start = (bf16[136,512]{1,0:T(8,128)(2,1)S(1)}, bf16[136,512]{1,0:T(8,128)(2,1)S(1)}, u32[]{:S(2)}, u32[]{:S(2)}) collective-permute-start(bf16[136,512]{1,0:T(8,128)(2,1)S(1)} %get-tuple-element.32), channel_id=1, source_target_pairs={{0,1},{1,2},{2,3},{3,0},{4,5},{5,6},{6,7},{7,4},{8,9},{9,10},{10,1... | collective-permute-start | bytes 417800 | tf_op jit(solution)/shard_map/ppermute | solution.py:270
  7.4 23.2 %collective-permute-start.1 = (bf16[136,512]{1,0:T(8,128)(2,1)S(1)}, bf16[136,512]{1,0:T(8,128)(2,1)S(1)}, u32[]{:S(2)}, u32[]{:S(2)}) collective-permute-start(bf16[136,512]{1,0:T(8,128)(2,1)S(1)} %get-tuple-element.31.refs_0_), channel_id=1, source_target_pairs={{0,2},{1,3},{2,0},{3,1},{4,6},{5,7},{6,4},{7,5},{8,10},{9,11},{10,... | collective-permute-start | bytes 417800 | tf_op jit(solution)/shard_map/ppermute | solution.py:270
  23.0 13.2 %collective-permute-start.4 = (bf16[2,136,512]{2,1,0:T(8,128)(2,1)S(1)}, bf16[2,136,512]{2,1,0:T(8,128)(2,1)S(1)}, u32[]{:S(2)}, u32[]{:S(2)}) collective-permute-start(bf16[2,136,512]{2,1,0:T(8,128)(2,1)S(1)} %shard_map.105), channel_id=1, source_target_pairs={{0,4},{4,8},{8,12},{12,16},{16,20},{20,24},{24,28},{1,5},{5,9},{9,... | collective-permute-start | bytes 835592 | tf_op jit(solution)/shard_map/ppermute | solution.py:275
  28.7 5.5 %collective-permute-start.3 = (bf16[1,136,512]{2,1,0:T(8,128)(2,1)S(1)}, bf16[1,136,512]{2,1,0:T(8,128)(2,1)S(1)}, u32[]{:S(2)}, u32[]{:S(2)}) collective-permute-start(bf16[1,136,512]{2,1,0:T(8,128)(2,1)S(1)} %shard_map.104), channel_id=1, source_target_pairs={{0,4},{4,8},{8,12},{12,16},{16,20},{20,24},{24,28},{1,5},{5,9},{9,... | collective-permute-start | bytes 417800 | tf_op jit(solution)/shard_map/ppermute | solution.py:275
  30.6 5.5 %collective-permute-start.5 = (bf16[1,136,512]{2,1,0:T(8,128)(2,1)S(1)}, bf16[1,136,512]{2,1,0:T(8,128)(2,1)S(1)}, u32[]{:S(2)}, u32[]{:S(2)}) collective-permute-start(bf16[1,136,512]{2,1,0:T(8,128)(2,1)S(1)} %shard_map.106), channel_id=1, source_target_pairs={{0,4},{4,8},{8,12},{12,16},{16,20},{20,24},{24,28},{1,5},{5,9},{9,... | collective-permute-start | bytes 417800 | tf_op jit(solution)/shard_map/ppermute | solution.py:275
  41.6 24.9 %collective-permute-start.7 = (bf16[256,1024]{1,0:T(8,128)(2,1)S(1)}, bf16[256,1024]{1,0:T(8,128)(2,1)S(1)}, u32[]{:S(2)}, u32[]{:S(2)}) collective-permute-start(bf16[256,1024]{1,0:T(8,128)(2,1)S(1)} %get-tuple-element.41), channel_id=1, source_target_pairs={{0,1},{1,0},{2,3},{3,2},{4,5},{5,4},{6,7},{7,6},{8,9},{9,8},{10,11... | collective-permute-start | bytes 1572872 | tf_op jit(solution)/shard_map/ppermute | solution.py:303
  41.7 9.3 %collective-permute-start.8 = (bf16[2,512,128]{2,1,0:T(8,128)(2,1)S(1)}, bf16[2,512,128]{2,1,0:T(8,128)(2,1)S(1)}, u32[]{:S(2)}, u32[]{:S(2)}) collective-permute-start(bf16[2,512,128]{2,1,0:T(8,128)(2,1)S(1)} %get-tuple-element.44), channel_id=1, source_target_pairs={{4,0},{8,4},{12,8},{16,12},{20,16},{24,20},{28,24},{5,1},{9,5},{13... | collective-permute-start | bytes 786440 | tf_op jit(solution)/shard_map/ppermute | solution.py:306
  45.0 9.9 %collective-permute-start.9 = (bf16[2,512,128]{2,1,0:T(8,128)(2,1)S(1)}, bf16[2,512,128]{2,1,0:T(8,128)(2,1)S(1)}, u32[]{:S(2)}, u32[]{:S(2)}) collective-permute-start(bf16[2,512,128]{2,1,0:T(8,128)(2,1)S(1)} %get-tuple-element.48), channel_id=1, source_target_pairs={{4,0},{8,4},{12,8},{16,12},{20,16},{24,20},{28,24},{5,1},{9,5},{13... | collective-permute-start | bytes 786440 | tf_op jit(solution)/shard_map/ppermute | solution.py:306
  51.1 9.9 %collective-permute-start.11 = (bf16[512,128]{1,0:T(8,128)(2,1)S(1)}, bf16[512,128]{1,0:T(8,128)(2,1)S(1)}, u32[]{:S(2)}, u32[]{:S(2)}) collective-permute-start(bf16[512,128]{1,0:T(8,128)(2,1)S(1)} %get-tuple-element.52), channel_id=1, source_target_pairs={{0,2},{1,3},{2,0},{3,1},{4,6},{5,7},{6,4},{7,5},{8,10},{9,11},{10,... | collective-permute-start | bytes 393224 | tf_op jit(solution)/shard_map/ppermute | solution.py:311
  54.9 6.3 %collective-permute-start.10 = (bf16[512,128]{1,0:T(8,128)(2,1)S(1)}, bf16[512,128]{1,0:T(8,128)(2,1)S(1)}, u32[]{:S(2)}, u32[]{:S(2)}) collective-permute-start(bf16[512,128]{1,0:T(8,128)(2,1)S(1)} %get-tuple-element.51), channel_id=1, source_target_pairs={{0,3},{1,0},{2,1},{3,2},{4,7},{5,4},{6,5},{7,6},{8,11},{9,8},{10,9... | collective-permute-start | bytes 393224 | tf_op jit(solution)/shard_map/ppermute | solution.py:311
  57.4 8.3 %collective-permute-start.12 = (bf16[512,128]{1,0:T(8,128)(2,1)S(1)}, bf16[512,128]{1,0:T(8,128)(2,1)S(1)}, u32[]{:S(2)}, u32[]{:S(2)}) collective-permute-start(bf16[512,128]{1,0:T(8,128)(2,1)S(1)} %get-tuple-element.53), channel_id=1, source_target_pairs={{0,1},{1,2},{2,3},{3,0},{4,5},{5,6},{6,7},{7,4},{8,9},{9,10},{10,1... | collective-permute-start | bytes 393224 | tf_op jit(solution)/shard_map/ppermute | solution.py:311

commit v4 on v3

--- a/solution.py
+++ b/solution.py
@@ -95,11 +95,13 @@
     far_pool, refs = entries(refs[: len(far_in)], far_in), refs[len(far_in) :]
     parts = group + len(far_out)
     if partner:
-        old, refs = refs[:parts], refs[parts:]
-        old = [*old[:group], *entries(old[group:], far_out)]
-    ag_ref, out, refs = refs[0], refs[1 : 1 + parts], refs[1 + parts :]
-    out = [*out[:group], *entries(out[group:], far_out)]
-    kv_s, seg_s, bias_s, term_s, p_s, dp_s, w_s, ds_s = refs
+        own_terms, refs = refs[0], refs[1:]
+        ag_ref, out, refs = refs[0], refs[1 : 1 + parts], refs[1 + parts :]
+        out = [*out[:group], *entries(out[group:], far_out)]
+        term_s, refs = refs[0], refs[1:]
+    else:
+        ag_ref, term_s, refs = refs[0], refs[1], refs[2:]
+    kv_s, seg_s, bias_s, p_s, dp_s, w_s, ds_s = refs
     slots, width, tile = term_s.shape
     half = width // 2
     size = half // heads
@@ -108,22 +110,25 @@
     scaling = size ** (-0.5)
     me = lax.axis_index("grp")
 
-    notes = pool[0][tile:, 0:tile]
+    def read(notes):
+        listed = [jnp.max(notes[1 + j : 2 + j, :]).astype(jnp.int32) for j in range(slots)]
+        count = jnp.max(notes[1 + slots : 2 + slots, :]).astype(jnp.int32)
+        found = []
+        for offset in (group, 0):
+            for d in range(group):
+                want = lax.rem(me - d + group, group) + offset
+                slot = jnp.int32(-1)
+                for j in range(slots):
+                    slot = jnp.where((listed[j] == want) & (j < count), j, slot)
+                found.append(slot)
+        return count, found
+
+    mine = pool[0][tile:, 0:tile].astype(F32)
+    notes = mine
     if partner:
         notes = jnp.where(parity() == 0, pool[group - 1][tile:, 0:tile], pool[1][tile:, 0:tile])
-    notes = notes.astype(F32)
-    listed = [jnp.max(notes[1 + j : 2 + j, :]).astype(jnp.int32) for j in range(slots)]
-    count = jnp.max(notes[1 + slots : 2 + slots, :]).astype(jnp.int32)
-
-    def slot_of(steps, offset):
-        want = lax.rem(me - steps + group, group) + offset
-        found = jnp.int32(-1)
-        for j in range(slots):
-            found = jnp.where((listed[j] == want) & (j < count), j, found)
-        return found
-
-    near_slot = [slot_of(d, group) for d in range(group)]
-    far_slot = [slot_of(d, 0) for d in range(group)]
+        notes = notes.astype(F32)
+    count, found = read(notes)
     for j in range(1, slots):
 
         @pl.when(j >= count)
@@ -131,7 +136,7 @@
             kv_s[j * tile : (j + 1) * tile, :] = jnp.zeros((tile, width), BF16)
             seg_s[j] = jnp.full(seg_s.shape[1:], -1.0, F32)
 
-    for slot, source in zip(near_slot + far_slot, [*pool, *far_pool]):
+    for slot, source in zip(found, [*pool, *far_pool]):
 
         @pl.when(slot >= 0)
         def _():
@@ -189,17 +194,26 @@
         weigh(h)
         finish(h)
 
-    for i, slot in enumerate(near_slot + far_slot):
-
-        @pl.when(slot >= 0)
-        def _():
-            new = term_s[slot].astype(F32)
-            out[i][...] = (new + old[i][...] if partner else new).astype(out[i].dtype)
-
-        @pl.when(slot < 0)
-        def _():
-            new = old[i][...] if partner else jnp.zeros((width, tile), F32)
-            out[i][...] = new.astype(out[i].dtype)
+    if not partner:
+        return
+    for slot, own_slot, target in zip(found, read(mine)[1], out):
+        here, there = term_s.at[jnp.maximum(slot, 0)], own_terms.at[jnp.maximum(own_slot, 0)]
+
+        @pl.when((slot >= 0) & (own_slot >= 0))
+        def _():
+            target[...] = (here[...].astype(F32) + there[...].astype(F32)).astype(target.dtype)
+
+        @pl.when((slot >= 0) & (own_slot < 0))
+        def _():
+            target[...] = here[...].astype(target.dtype)
+
+        @pl.when((slot < 0) & (own_slot >= 0))
+        def _():
+            target[...] = there[...].astype(target.dtype)
+
+        @pl.when((slot < 0) & (own_slot < 0))
+        def _():
+            target[...] = jnp.zeros((width, tile), target.dtype)
 
 
 def join_kernel(far, *refs):
@@ -273,7 +287,7 @@
     qg_partner = lax.ppermute(qg_other, "grp", partners)
     far_in = [g for g in ([0], first, rest) if g]
     far = [lax.ppermute(merge([near[d] for d in g]), "cp", ahead) for g in far_in]
-    far_out = [g for g in (first, [0] + rest) if g]
+    far_out = [g for g in (rest + first[1:], first[:1] + [0]) if g]
 
     ag = shape((2 * tile, full // PAIR), BF16)
     term = shape((width, tile), F32)
@@ -281,7 +295,6 @@
         pltpu.VMEM((slots * tile, width), BF16),
         pltpu.VMEM((slots, payload.shape[0] - tile, tile), F32),
         pltpu.VMEM((tile, slots * tile), F32),
-        pltpu.VMEM((slots, width, tile), BF16),
         pltpu.VMEM((heads, rows, slots * tile), F32),
         pltpu.VMEM((heads, rows, slots * tile), F32),
         pltpu.VMEM((heads, rows, slots * tile), BF16),
@@ -289,17 +302,19 @@
     ]
     flops = 12 * heads * rows * slots * tile * size
 
-    def attend(qg, before, dtype):
+    def attend(partner, qg, outs, extra, extra_scratch):
         return call(
-            functools.partial(attend_kernel, heads, group, far_in, far_out, bool(before)),
-            [ag] + [term] * group + [shape((len(g), width, tile), dtype) for g in far_out],
-            [qg, *near, *far, *before],
-            scratch=scratch,
+            functools.partial(attend_kernel, heads, group, far_in, far_out, partner),
+            [ag, *outs],
+            [qg, *near, *far, *extra],
+            scratch=extra_scratch + scratch,
             flops=flops,
         )
 
-    ag_mine, *terms = attend(qg_mine, [], F32)
-    ag_partner, *terms = attend(qg_partner, terms, BF16)
+    listed = (slots, width, tile)
+    ag_mine, own_terms = attend(False, qg_mine, [shape(listed, BF16)], [], [])
+    outs = [term] * group + [shape((len(g), width, tile), BF16) for g in far_out]
+    ag_partner, *terms = attend(True, qg_partner, outs, [own_terms], [pltpu.VMEM(listed, BF16)])
     ag_back = lax.ppermute(ag_partner, "grp", partners)
     joined = {}
     for g, far_terms in zip(far_out, terms[group:]):

time: 67.8 us -> 68 us (level)
  the two profiles are of different devices: /device:TPU:3 before, /device:TPU:5 now
where the time goes in v4:
time: 68 us; the launch traced here: 67.7 us
  starting transfers between devices  28.9 us (42%)
  waiting for transfers between devices  27.6 us (41%)
  Pallas kernels  9.84 us (14%)
  between operations  1.41 us (2%)
    ppermute x3, waiting for transfers between devices, body(): near.append(lax.ppermute(other if d % PAIR else mine, 'grp', ring(d)))  14 us
    pallas_call x11, Pallas kernels, call(): pl.pallas_call(kernel, out_shape=outs, in_specs=in_specs or [VMEM] * len(...  9.84 us
    ppermute x3, starting transfers between devices, body(): lax.ppermute(merge([near[d] for d in g]), 'cp', ahead)  9.51 us
    ppermute x3, waiting for transfers between devices, body(): sums.append(lax.ppermute(joined[d], 'grp', ring(-d)))  8.26 us
    ppermute x2, starting transfers between devices, body(): later = lax.ppermute(far_terms, 'cp', back)  7.15 us
    ppermute x3, starting transfers between devices, body(): sums.append(lax.ppermute(joined[d], 'grp', ring(-d)))  6.99 us
    ppermute x3, starting transfers between devices, body(): near.append(lax.ppermute(other if d % PAIR else mine, 'grp', ring(d)))  3.83 us
    ppermute x2, waiting for transfers between devices, body(): later = lax.ppermute(far_terms, 'cp', back)  2.75 us
  transfers between devices with their start and end apart: 13, of which 7 were waited for; matrix products, arithmetic and copies ran while one was open for 0% of the time, Pallas kernels for 7%

profile of v4, /device:TPU:5, one launch (start us, length us, event | category | flops | bytes accessed | tf_op | source)
XLA Modules:
  0.0 67.7 jit_solution(17431822972477304713)
XLA Ops:
  0.6 1.5 %shard_map.102 = (bf16[2048,128]{1,0:T(8,128)(2,1)S(1)}, bf16[2048,128]{1,0:T(8,128)(2,1)S(1)}) custom-call(bf16[128,2048]{1,0:T(8,128)(2,1)} %q_ref.1, bf16[128,2048]{1,0:T(8,128)(2,1)} %g_ref.1), custom_call_target="tpu_custom_call" | custom-call | bytes 2097152 | tf_op jit(solution)/shard_map/pallas_call | solution.py:26
  2.1 1.4 %collective-permute-start.6 = (bf16[2048,128]{1,0:T(8,128)(2,1)S(1)}, bf16[2048,128]{1,0:T(8,128)(2,1)S(1)}, u32[]{:S(2)}, u32[]{:S(2)}) collective-permute-start(bf16[2048,128]{1,0:T(8,128)(2,1)S(1)} %get-tuple-element.29), channel_id=1, source_target_pairs={{0,1},{1,0},{2,3},{3,2},{4,5},{5,4},{6,7},{7,6},{8,9},{9,8},{10,11... | collective-permute-start | bytes 1572872 | tf_op jit(solution)/shard_map/ppermute | solution.py:287
  4.1 1.0 %shard_map.103 = (bf16[136,512]{1,0:T(8,128)(2,1)S(1)}, bf16[136,512]{1,0:T(8,128)(2,1)S(1)}) custom-call(s32[1,4]{1,0:T(1,128)} %ids_ref.1, s32[1]{0:T(128)S(6)} %copy.11.count_ref, bf16[128,512]{1,0:T(8,128)(2,1)} %k_ref.1, bf16[128,512]{1,0:T(8,128)(2,1)} %v_ref.1, s32[1,128]{1,0:T(1,128)} %bitcast.1), custom_call_target="tpu_custom_call" | custom-call | bytes 541204 | tf_op jit(solution)/shard_map/pallas_call | solution.py:26
  5.1 2.2 %collective-permute-start.2 = (bf16[136,512]{1,0:T(8,128)(2,1)S(1)}, bf16[136,512]{1,0:T(8,128)(2,1)S(1)}, u32[]{:S(2)}, u32[]{:S(2)}) collective-permute-start(bf16[136,512]{1,0:T(8,128)(2,1)S(1)} %get-tuple-element.27), channel_id=1, source_target_pairs={{0,3},{1,0},{2,1},{3,2},{4,7},{5,4},{6,5},{7,6},{8,11},{9,8},{10,9... | collective-permute-start | bytes 417800 | tf_op jit(solution)/shard_map/ppermute | solution.py:284
  7.4 0.0 collective-permute-start
  7.4 1.6 %collective-permute-start.1 = (bf16[136,512]{1,0:T(8,128)(2,1)S(1)}, bf16[136,512]{1,0:T(8,128)(2,1)S(1)}, u32[]{:S(2)}, u32[]{:S(2)}) collective-permute-start(bf16[136,512]{1,0:T(8,128)(2,1)S(1)} %get-tuple-element.26.refs_0_), channel_id=1, source_target_pairs={{0,2},{1,3},{2,0},{3,1},{4,6},{5,7},{6,4},{7,5},{8,10},{9,11},{10,... | collective-permute-start | bytes 417800 | tf_op jit(solution)/shard_map/ppermute | solution.py:284
  9.0 12.9 %collective-permute-done.2.refs_1_.refs_3_ = bf16[136,512]{1,0:T(8,128)(2,1)S(1)} collective-permute-done((bf16[136,512]{1,0:T(8,128)(2,1)S(1)}, bf16[136,512]{1,0:T(8,128)(2,1)S(1)}, u32[]{:S(2)}, u32[]{:S(2)}) %collective-permute-start.2) | collective-permute-done | bytes 139296 | tf_op jit(solution)/shard_map/ppermute | solution.py:284
  21.9 1.1 %collective-permute-done.refs_0_.refs_1_ = bf16[136,512]{1,0:T(8,128)(2,1)S(1)} collective-permute-done((bf16[136,512]{1,0:T(8,128)(2,1)S(1)}, bf16[136,512]{1,0:T(8,128)(2,1)S(1)}, u32[]{:S(2)}, u32[]{:S(2)}) %collective-permute-start) | collective-permute-done | bytes 139296 | tf_op jit(solution)/shard_map/ppermute | solution.py:284
  23.0 5.7 %collective-permute-start.4 = (bf16[2,136,512]{2,1,0:T(8,128)(2,1)S(1)}, bf16[2,136,512]{2,1,0:T(8,128)(2,1)S(1)}, u32[]{:S(2)}, u32[]{:S(2)}) collective-permute-start(bf16[2,136,512]{2,1,0:T(8,128)(2,1)S(1)} %shard_map.105), channel_id=1, source_target_pairs={{0,4},{4,8},{8,12},{12,16},{16,20},{20,24},{24,28},{1,5},{5,9},{9,... | collective-permute-start | bytes 835592 | tf_op jit(solution)/shard_map/ppermute | solution.py:289
  28.7 1.9 %collective-permute-start.3 = (bf16[1,136,512]{2,1,0:T(8,128)(2,1)S(1)}, bf16[1,136,512]{2,1,0:T(8,128)(2,1)S(1)}, u32[]{:S(2)}, u32[]{:S(2)}) collective-permute-start(bf16[1,136,512]{2,1,0:T(8,128)(2,1)S(1)} %shard_map.104), channel_id=1, source_target_pairs={{0,4},{4,8},{8,12},{12,16},{16,20},{20,24},{24,28},{1,5},{5,9},{9,... | collective-permute-start | bytes 417800 | tf_op jit(solution)/shard_map/ppermute | solution.py:289
  30.6 0.0 collective-permute-done.1.refs_0_.refs_2_
  30.6 1.9 %collective-permute-start.5 = (bf16[1,136,512]{2,1,0:T(8,128)(2,1)S(1)}, bf16[1,136,512]{2,1,0:T(8,128)(2,1)S(1)}, u32[]{:S(2)}, u32[]{:S(2)}) collective-permute-start(bf16[1,136,512]{2,1,0:T(8,128)(2,1)S(1)} %shard_map.106), channel_id=1, source_target_pairs={{0,4},{4,8},{8,12},{12,16},{16,20},{20,24},{24,28},{1,5},{5,9},{9,... | collective-permute-start | bytes 417800 | tf_op jit(solution)/shard_map/ppermute | solution.py:289
  32.6 1.1 %collective-permute-done.3.refs_4_ = bf16[1,136,512]{2,1,0:T(8,128)(2,1)S(1)} collective-permute-done((bf16[1,136,512]{2,1,0:T(8,128)(2,1)S(1)}, bf16[1,136,512]{2,1,0:T(8,128)(2,1)S(1)}, u32[]{:S(2)}, u32[]{:S(2)}) %collective-permute-start.3) | collective-permute-done | bytes 139296 | tf_op jit(solution)/shard_map/ppermute | solution.py:289
  33.6 1.5 %collective-permute-done.5.refs_6_ = bf16[1,136,512]{2,1,0:T(8,128)(2,1)S(1)} collective-permute-done((bf16[1,136,512]{2,1,0:T(8,128)(2,1)S(1)}, bf16[1,136,512]{2,1,0:T(8,128)(2,1)S(1)}, u32[]{:S(2)}, u32[]{:S(2)}) %collective-permute-start.5) | collective-permute-done | bytes 139296 | tf_op jit(solution)/shard_map/ppermute | solution.py:289
  35.1 0.0 collective-permute-done.4.refs_5_
  35.1 2.5 %shard_map.107 = (bf16[256,1024]{1,0:T(8,128)(2,1)S(1)}, bf16[4,512,128]{2,1,0:T(8,128)(2,1)S(1)}) custom-call(bf16[2048,128]{1,0:T(8,128)(2,1)S(1)} %get-tuple-element.25.qg_ref, bf16[136,512]{1,0:T(8,128)(2,1)S(1)} %get-tuple-element.26.refs_0_, bf16[136,512]{1,0:T(8,128)(2,1)S(1)} %collective-permute-done.refs_0_.refs_1_, ...), custom_call_target="tpu_custom_call" | custom-call | flops 805306368 | bytes 2686976 | tf_op jit(solution)/shard_map/pallas_call | solution.py:26
  37.6 0.0 collective-permute-done.6.qg_ref
  37.7 2.8 %shard_map.108 = (bf16[256,1024]{1,0:T(8,128)(2,1)S(1)}, f32[512,128]{1,0:T(8,128)S(1)}, f32[512,128]{1,0:T(8,128)S(1)}, f32[512,128]{1,0:T(8,128)S(1)}, f32[512...) custom-call(bf16[2048,128]{1,0:T(8,128)(2,1)S(1)} %collective-permute-done.6.qg_ref, ...), custom_call_target="tpu_custom_call" | custom-call | flops 805306368 | bytes 4259840 | tf_op jit(solution)/shard_map/pallas_call | solution.py:26
  40.5 0.1 collective-permute-start.7
  40.6 5.2 %collective-permute-start.8 = (bf16[2,512,128]{2,1,0:T(8,128)(2,1)S(1)}, bf16[2,512,128]{2,1,0:T(8,128)(2,1)S(1)}, u32[]{:S(2)}, u32[]{:S(2)}) collective-permute-start(bf16[2,512,128]{2,1,0:T(8,128)(2,1)S(1)} %get-tuple-element.34), channel_id=1, source_target_pairs={{4,0},{8,4},{12,8},{16,12},{20,16},{24,20},{28,24},{5,1},{9,5},{13... | collective-permute-start | bytes 786440 | tf_op jit(solution)/shard_map/ppermute | solution.py:321
  45.8 1.9 %collective-permute-start.10 = (bf16[2,512,128]{2,1,0:T(8,128)(2,1)S(1)}, bf16[2,512,128]{2,1,0:T(8,128)(2,1)S(1)}, u32[]{:S(2)}, u32[]{:S(2)}) collective-permute-start(bf16[2,512,128]{2,1,0:T(8,128)(2,1)S(1)} %get-tuple-element.39), channel_id=1, source_target_pairs={{4,0},{8,4},{12,8},{16,12},{20,16},{24,20},{28,24},{5,1},{9,5},{13... | collective-permute-start | bytes 786440 | tf_op jit(solution)/shard_map/ppermute | solution.py:321
  47.7 1.6 %collective-permute-done.8.far = bf16[2,512,128]{2,1,0:T(8,128)(2,1)S(1)} collective-permute-done((bf16[2,512,128]{2,1,0:T(8,128)(2,1)S(1)}, bf16[2,512,128]{2,1,0:T(8,128)(2,1)S(1)}, u32[]{:S(2)}, u32[]{:S(2)}) %collective-permute-start.8) | collective-permute-done | bytes 262176 | tf_op jit(solution)/shard_map/ppermute | solution.py:321
  49.3 3.3 %collective-permute-start.9 = (bf16[512,128]{1,0:T(8,128)(2,1)S(1)}, bf16[512,128]{1,0:T(8,128)(2,1)S(1)}, u32[]{:S(2)}, u32[]{:S(2)}) collective-permute-start(bf16[512,128]{1,0:T(8,128)(2,1)S(1)} %get-tuple-element.38), channel_id=1, source_target_pairs={{0,3},{1,0},{2,1},{3,2},{4,7},{5,4},{6,5},{7,6},{8,11},{9,8},{10,9... | collective-permute-start | bytes 393224 | tf_op jit(solution)/shard_map/ppermute | solution.py:326
  52.6 1.2 %collective-permute-done.10.far = bf16[2,512,128]{2,1,0:T(8,128)(2,1)S(1)} collective-permute-done((bf16[2,512,128]{2,1,0:T(8,128)(2,1)S(1)}, bf16[2,512,128]{2,1,0:T(8,128)(2,1)S(1)}, u32[]{:S(2)}, u32[]{:S(2)}) %collective-permute-start.10) | collective-permute-done | bytes 262176 | tf_op jit(solution)/shard_map/ppermute | solution.py:321
  53.8 3.7 %collective-permute-start.11 = (bf16[512,128]{1,0:T(8,128)(2,1)S(1)}, bf16[512,128]{1,0:T(8,128)(2,1)S(1)}, u32[]{:S(2)}, u32[]{:S(2)}) collective-permute-start(bf16[512,128]{1,0:T(8,128)(2,1)S(1)} %get-tuple-element.42), channel_id=1, source_target_pairs={{0,2},{1,3},{2,0},{3,1},{4,6},{5,7},{6,4},{7,5},{8,10},{9,11},{10,... | collective-permute-start | bytes 393224 | tf_op jit(solution)/shard_map/ppermute | solution.py:326
  57.6 0.0 collective-permute-start.12
  57.6 0.0 collective-permute-done.9.refs_1_
  57.6 8.3 %collective-permute-done.11.refs_2_ = bf16[512,128]{1,0:T(8,128)(2,1)S(1)} collective-permute-done((bf16[512,128]{1,0:T(8,128)(2,1)S(1)}, bf16[512,128]{1,0:T(8,128)(2,1)S(1)}, u32[]{:S(2)}, u32[]{:S(2)}) %collective-permute-start.11) | collective-permute-done | bytes 131104 | tf_op jit(solution)/shard_map/ppermute | solution.py:326
  65.8 0.0 collective-permute-done.12.refs_3_
  65.8 0.8 %shard_map.112 = (bf16[128,512]{1,0:T(8,128)(2,1)}, bf16[128,512]{1,0:T(8,128)(2,1)}) custom-call(f32[512,128]{1,0:T(8,128)S(1)} %get-tuple-element.37.refs_0_, bf16[512,128]{1,0:T(8,128)(2,1)S(1)} %collective-permute-done.9.refs_1_, bf16[512,128]{1,0:T(8,128)(2,1)S(1)} %collective-permute-done.11.refs_2_, bf16[512,128]{1,0:T(8,128)(2,1)S(1)} %collective-permute-done.12.refs_3_), custom_call_target="tpu_custom_call" | custom-call | bytes 917504 | tf_op jit(solution)/shard_map/pallas_call | solution.py:26
  66.7 0.0 collective-permute-done.7.other_ref
  66.7 1.0 %shard_map.109 = (bf16[128,2048]{1,0:T(8,128)(2,1)}, bf16[128,2048]{1,0:T(8,128)(2,1)}) custom-call(bf16[256,1024]{1,0:T(8,128)(2,1)S(1)} %get-tuple-element.28.mine_ref, bf16[256,1024]{1,0:T(8,128)(2,1)S(1)} %collective-permute-done.7.other_ref), custom_call_target="tpu_custom_call" | custom-call | bytes 2097152 | tf_op jit(solution)/shard_map/pallas_call | solution.py:26
  (5 shorter events, 0.1 us)
Async XLA Ops:
  2.1 35.5 %collective-permute-start.6 = (bf16[2048,128]{1,0:T(8,128)(2,1)S(1)}, bf16[2048,128]{1,0:T(8,128)(2,1)S(1)}, u32[]{:S(2)}, u32[]{:S(2)}) collective-permute-start(bf16[2048,128]{1,0:T(8,128)(2,1)S(1)} %get-tuple-element.29), channel_id=1, source_target_pairs={{0,1},{1,0},{2,3},{3,2},{4,5},{5,4},{6,7},{7,6},{8,9},{9,8},{10,11... | collective-permute-start | bytes 1572872 | tf_op jit(solution)/shard_map/ppermute | solution.py:287
  5.1 16.8 %collective-permute-start.2 = (bf16[136,512]{1,0:T(8,128)(2,1)S(1)}, bf16[136,512]{1,0:T(8,128)(2,1)S(1)}, u32[]{:S(2)}, u32[]{:S(2)}) collective-permute-start(bf16[136,512]{1,0:T(8,128)(2,1)S(1)} %get-tuple-element.27), channel_id=1, source_target_pairs={{0,3},{1,0},{2,1},{3,2},{4,7},{5,4},{6,5},{7,6},{8,11},{9,8},{10,9... | collective-permute-start | bytes 417800 | tf_op jit(solution)/shard_map/ppermute | solution.py:284
  7.4 15.6 %collective-permute-start = (bf16[136,512]{1,0:T(8,128)(2,1)S(1)}, bf16[136,512]{1,0:T(8,128)(2,1)S(1)}, u32[]{:S(2)}, u32[]{:S(2)}) collective-permute-start(bf16[136,512]{1,0:T(8,128)(2,1)S(1)} %get-tuple-element.27), channel_id=1, source_target_pairs={{0,1},{1,2},{2,3},{3,0},{4,5},{5,6},{6,7},{7,4},{8,9},{9,10},{10,1... | collective-permute-start | bytes 417800 | tf_op jit(solution)/shard_map/ppermute | solution.py:284
  7.4 23.2 %collective-permute-start.1 = (bf16[136,512]{1,0:T(8,128)(2,1)S(1)}, bf16[136,512]{1,0:T(8,128)(2,1)S(1)}, u32[]{:S(2)}, u32[]{:S(2)}) collective-permute-start(bf16[136,512]{1,0:T(8,128)(2,1)S(1)} %get-tuple-element.26.refs_0_), channel_id=1, source_target_pairs={{0,2},{1,3},{2,0},{3,1},{4,6},{5,7},{6,4},{7,5},{8,10},{9,11},{10,... | collective-permute-start | bytes 417800 | tf_op jit(solution)/shard_map/ppermute | solution.py:284
  23.0 12.1 %collective-permute-start.4 = (bf16[2,136,512]{2,1,0:T(8,128)(2,1)S(1)}, bf16[2,136,512]{2,1,0:T(8,128)(2,1)S(1)}, u32[]{:S(2)}, u32[]{:S(2)}) collective-permute-start(bf16[2,136,512]{2,1,0:T(8,128)(2,1)S(1)} %shard_map.105), channel_id=1, source_target_pairs={{0,4},{4,8},{8,12},{12,16},{16,20},{20,24},{24,28},{1,5},{5,9},{9,... | collective-permute-start | bytes 835592 | tf_op jit(solution)/shard_map/ppermute | solution.py:289
  28.7 4.9 %collective-permute-start.3 = (bf16[1,136,512]{2,1,0:T(8,128)(2,1)S(1)}, bf16[1,136,512]{2,1,0:T(8,128)(2,1)S(1)}, u32[]{:S(2)}, u32[]{:S(2)}) collective-permute-start(bf16[1,136,512]{2,1,0:T(8,128)(2,1)S(1)} %shard_map.104), channel_id=1, source_target_pairs={{0,4},{4,8},{8,12},{12,16},{16,20},{20,24},{24,28},{1,5},{5,9},{9,... | collective-permute-start | bytes 417800 | tf_op jit(solution)/shard_map/ppermute | solution.py:289
  30.6 4.5 %collective-permute-start.5 = (bf16[1,136,512]{2,1,0:T(8,128)(2,1)S(1)}, bf16[1,136,512]{2,1,0:T(8,128)(2,1)S(1)}, u32[]{:S(2)}, u32[]{:S(2)}) collective-permute-start(bf16[1,136,512]{2,1,0:T(8,128)(2,1)S(1)} %shard_map.106), channel_id=1, source_target_pairs={{0,4},{4,8},{8,12},{12,16},{16,20},{20,24},{24,28},{1,5},{5,9},{9,... | collective-permute-start | bytes 417800 | tf_op jit(solution)/shard_map/ppermute | solution.py:289
  40.5 26.2 %collective-permute-start.7 = (bf16[256,1024]{1,0:T(8,128)(2,1)S(1)}, bf16[256,1024]{1,0:T(8,128)(2,1)S(1)}, u32[]{:S(2)}, u32[]{:S(2)}) collective-permute-start(bf16[256,1024]{1,0:T(8,128)(2,1)S(1)} %get-tuple-element.31), channel_id=1, source_target_pairs={{0,1},{1,0},{2,3},{3,2},{4,5},{5,4},{6,7},{7,6},{8,9},{9,8},{10,11... | collective-permute-start | bytes 1572872 | tf_op jit(solution)/shard_map/ppermute | solution.py:318
  40.6 8.7 %collective-permute-start.8 = (bf16[2,512,128]{2,1,0:T(8,128)(2,1)S(1)}, bf16[2,512,128]{2,1,0:T(8,128)(2,1)S(1)}, u32[]{:S(2)}, u32[]{:S(2)}) collective-permute-start(bf16[2,512,128]{2,1,0:T(8,128)(2,1)S(1)} %get-tuple-element.34), channel_id=1, source_target_pairs={{4,0},{8,4},{12,8},{16,12},{20,16},{24,20},{28,24},{5,1},{9,5},{13... | collective-permute-start | bytes 786440 | tf_op jit(solution)/shard_map/ppermute | solution.py:321
  45.8 8.0 %collective-permute-start.10 = (bf16[2,512,128]{2,1,0:T(8,128)(2,1)S(1)}, bf16[2,512,128]{2,1,0:T(8,128)(2,1)S(1)}, u32[]{:S(2)}, u32[]{:S(2)}) collective-permute-start(bf16[2,512,128]{2,1,0:T(8,128)(2,1)S(1)} %get-tuple-element.39), channel_id=1, source_target_pairs={{4,0},{8,4},{12,8},{16,12},{20,16},{24,20},{28,24},{5,1},{9,5},{13... | collective-permute-start | bytes 786440 | tf_op jit(solution)/shard_map/ppermute | solution.py:321
  49.3 8.2 %collective-permute-start.9 = (bf16[512,128]{1,0:T(8,128)(2,1)S(1)}, bf16[512,128]{1,0:T(8,128)(2,1)S(1)}, u32[]{:S(2)}, u32[]{:S(2)}) collective-permute-start(bf16[512,128]{1,0:T(8,128)(2,1)S(1)} %get-tuple-element.38), channel_id=1, source_target_pairs={{0,3},{1,0},{2,1},{3,2},{4,7},{5,4},{6,5},{7,6},{8,11},{9,8},{10,9... | collective-permute-start | bytes 393224 | tf_op jit(solution)/shard_map/ppermute | solution.py:326
  53.8 12.0 %collective-permute-start.11 = (bf16[512,128]{1,0:T(8,128)(2,1)S(1)}, bf16[512,128]{1,0:T(8,128)(2,1)S(1)}, u32[]{:S(2)}, u32[]{:S(2)}) collective-permute-start(bf16[512,128]{1,0:T(8,128)(2,1)S(1)} %get-tuple-element.42), channel_id=1, source_target_pairs={{0,2},{1,3},{2,0},{3,1},{4,6},{5,7},{6,4},{7,5},{8,10},{9,11},{10,... | collective-permute-start | bytes 393224 | tf_op jit(solution)/shard_map/ppermute | solution.py:326
  57.6 8.3 %collective-permute-start.12 = (bf16[512,128]{1,0:T(8,128)(2,1)S(1)}, bf16[512,128]{1,0:T(8,128)(2,1)S(1)}, u32[]{:S(2)}, u32[]{:S(2)}) collective-permute-start(bf16[512,128]{1,0:T(8,128)(2,1)S(1)} %get-tuple-element.43), channel_id=1, source_target_pairs={{0,1},{1,2},{2,3},{3,0},{4,5},{5,6},{6,7},{7,4},{8,9},{9,10},{10,1... | collective-permute-start | bytes 393224 | tf_op jit(solution)/shard_map/ppermute | solution.py:326
